TPU v7x, 32 devices: a whole 2x2x4 slice. The times are simulated.
32 devices in a mesh: wide: 16 (over z, y, x), narrow: 2 (over core).
Axes of the slice: x: 2, y: 2, z: 4, core: 2. Of those that a mesh axis runs over, the one named last changes fastest.
Arguments:
- electric: float32 [3, 3, 128, 48, 128], P(None, None, 'wide', 'narrow'), may hold values from -6 to 6
- magnetic: float32 [3, 3, 128, 48, 128], P(None, None, 'wide', 'narrow'), may hold values from -6 to 6
- current: float32 [3, 128, 48, 128], P(None, 'wide', 'narrow'), may hold values from -6 to 6
- density_tiles: float32 [64, 24, 64], P('wide', 'narrow'), may hold values from 0 to 1
- tile_slabs: int32 [16], replicated, may hold values from 0 to 15, each once
- design_box: int32 [6], replicated, may hold values from 0 to 128, as said below
- material_mask: int32 [128, 48, 128], P('wide', 'narrow'), may hold values 0 or 1
- material_levels: float32 [2], replicated, may hold values from 2 to 12
Outputs:
- final_electric: float32 [3, 3, 128, 48, 128], P(None, None, 'wide', 'narrow')
- final_magnetic: float32 [3, 3, 128, 48, 128], P(None, None, 'wide', 'narrow')
Inputs may be any that keep to these rules, and one draw needn't show every extreme that they name: `tile_slabs`: each slab index appears exactly once. `design_box`: along each dimension of n cells the low bound is below n // 4; the high bound is 128 along the first dimension, at least 24 along the second, and at least n // 2 along the third.
All inputs are finite; a program needn't handle non-finite values. No bound on the sum of `material_mask` on one device may be relied on, other than what follows from the above.
Results may differ from a plain program's by a relative error of at most 0.00013.
Values sent between devices are 32-bit elements; how exact they have to be, the bound alone decides.
A program may use at most 64 MiB of HBM per device.

v0:
```python
import functools
import math

import jax
import jax.numpy as jnp
from jax import lax
from jax.experimental import pallas as pl
from jax.experimental.pallas import tpu as pltpu
from jax.sharding import PartitionSpec as P

STEPS = 4
sharpness = 8.0
thresholds = (0.7, 0.5, 0.3)
time_step = 0.5

PAD = 8
MESH = pl.DeviceIdType.MESH
UP, DOWN, RIGHT, LEFT, DIAG_A, DIAG_B, UP_H = range(7)


def refine_weights(rows, columns, offset, cells):
    k = lax.broadcasted_iota(jnp.int32, (rows, columns), 0) - offset
    j = lax.broadcasted_iota(jnp.int32, (rows, columns), 1)
    return _weights(k, j, cells)


def _weights(k, j, last):
    cell = j >> 1
    odd = (j & 1) == 1
    here = jnp.where(k == cell, jnp.where(odd, 0.5, 1.0), 0.0)
    above = jnp.where(odd & (k == jnp.minimum(cell + 1, last)), 0.5, 0.0)
    return here + above


def exact_dot(a, b):
    return jnp.dot(a, b, precision=lax.Precision.HIGHEST, preferred_element_type=jnp.float32)


def kernel(
    W,
    N,
    slabs,
    box,
    levels,
    e_in,
    h_in,
    j_in,
    tiles_in,
    mask_in,
    e_out,
    h_out,
    E,
    H,
    J,
    tile,
    mask,
    coef,
    gathered,
    unpacked,
    coarse,
    row_send,
    row_recv,
    xlo,
    xlo_h,
    xhi,
    s_right,
    r_right,
    s_left,
    r_left,
    r_diag_a,
    r_diag_b,
    h_row,
    load_sem,
    out_sem,
    send_sem,
    recv_sem,
    tile_send,
    tile_recv,
    row_sems,
):
    w = lax.axis_index("wide")
    n = lax.axis_index("narrow")
    R, _, X, _, Z = e_out.shape
    Y = e_out.shape[3]
    HY, TR, HZ = tiles_in.shape
    own_x = pl.ds(1, X)
    own_y = pl.ds(PAD, Y)

    loads = [
        pltpu.make_async_copy(tiles_in, tile, load_sem.at[0]),
        pltpu.make_async_copy(e_in, E.at[:, :, own_x, own_y, :], load_sem.at[1]),
        pltpu.make_async_copy(h_in, H.at[:, :, own_x, own_y, :], load_sem.at[2]),
        pltpu.make_async_copy(j_in, J, load_sem.at[3]),
        pltpu.make_async_copy(mask_in, mask, load_sem.at[4]),
    ]
    for load in loads:
        load.start()

    has_up = w < W - 1
    has_down = w > 0
    has_right = n < N - 1
    has_left = n > 0

    barrier = pltpu.get_barrier_semaphore()

    @pl.loop(1, W)
    def _(d):
        pl.semaphore_signal(
            barrier, inc=1, device_id=(lax.rem(w + d, W), n), device_id_type=MESH
        )

    others = (
        (has_right, w, n + 1),
        (has_left, w, n - 1),
        (has_down & has_right, w - 1, n + 1),
        (has_up & has_left, w + 1, n - 1),
    )
    expected = W - 1
    for there, to_w, to_n in others:
        expected = expected + there.astype(jnp.int32)

        @pl.when(there)
        def _():
            pl.semaphore_signal(barrier, inc=1, device_id=(to_w, to_n), device_id_type=MESH)

    zero_plane = jnp.zeros((Y + 2 * PAD, Z), jnp.float32)
    zero_tile = jnp.zeros((PAD, Z), jnp.float32)

    @pl.loop(0, R)
    def _(r):
        for c in range(3):
            E[r, c, 0] = zero_plane
            E[r, c, X + 1] = zero_plane
            H[r, c, 0] = zero_plane
            for p in range(1, X + 1):
                E[r, c, p, pl.ds(PAD + Y, PAD), :] = zero_tile
                H[r, c, p, pl.ds(0, PAD), :] = zero_tile
        h_row[r] = jnp.zeros((2, X, Z), jnp.float32)

    half = TR // 2
    loads[0].wait()
    for p in range(half):
        gathered[w, pl.ds(p * HY, HY), :] = jnp.concatenate(
            [tile[:, p, :], tile[:, p + half, :]], axis=-1
        )

    pl.semaphore_wait(barrier, expected)

    def tile_copy(d):
        return pltpu.make_async_remote_copy(
            src_ref=gathered.at[w],
            dst_ref=gathered.at[w],
            send_sem=tile_send.at[d],
            recv_sem=tile_recv.at[d],
            device_id=(lax.rem(w + d, W), n),
            device_id_type=MESH,
        )

    def messages(s, r):
        def copy(kind, src, dst, to_w, to_n):
            return pltpu.make_async_remote_copy(
                src_ref=src,
                dst_ref=dst,
                send_sem=send_sem.at[s, r, kind],
                recv_sem=recv_sem.at[s, r, kind],
                device_id=(to_w, to_n),
                device_id_type=MESH,
            )

        rows = 5 if s == 0 else 3
        found = [
            (has_up, has_down, copy(UP, E.at[r, :, X, own_y, :], xlo.at[s, r], w + 1, n)),
            (
                has_down,
                has_up,
                copy(DOWN, E.at[r, pl.ds(1, 2), 1, own_y, :], xhi.at[s, r], w - 1, n),
            ),
            (
                has_right,
                has_left,
                copy(
                    RIGHT,
                    s_right.at[s, r, pl.ds(0, rows)],
                    r_right.at[s, r, pl.ds(0, rows)],
                    w,
                    n + 1,
                ),
            ),
            (has_left, has_right, copy(LEFT, s_left.at[s, r], r_left.at[s, r], w, n - 1)),
            (
                has_down & has_right,
                has_up & has_left,
                copy(
                    DIAG_A, E.at[r, 1, 1, pl.ds(Y, PAD), :], r_diag_a.at[s, r], w - 1, n + 1
                ),
            ),
            (
                has_up & has_left,
                has_down & has_right,
                copy(
                    DIAG_B, E.at[r, 0, X, pl.ds(PAD, PAD), :], r_diag_b.at[s, r], w + 1, n - 1
                ),
            ),
        ]
        if s == 0:
            found.append(
                (
                    has_up,
                    has_down,
                    copy(UP_H, H.at[r, pl.ds(1, 2), X, own_y, :], xlo_h.at[r], w + 1, n),
                )
            )
        return found

    def send(s, r):
        for p in range(X):
            for c in range(3):
                s_right[s, r, c, pl.ds(p, 1), :] = E[r, c, p + 1, pl.ds(PAD + Y - 1, 1), :]
            if s == 0:
                s_right[s, r, 3, pl.ds(p, 1), :] = H[r, 0, p + 1, pl.ds(PAD + Y - 1, 1), :]
                s_right[s, r, 4, pl.ds(p, 1), :] = H[r, 2, p + 1, pl.ds(PAD + Y - 1, 1), :]
            s_left[s, r, 0, pl.ds(p, 1), :] = E[r, 0, p + 1, pl.ds(PAD, 1), :]
            s_left[s, r, 1, pl.ds(p, 1), :] = E[r, 2, p + 1, pl.ds(PAD, 1), :]
        for sends, _, copy in messages(s, r):
            pl.when(sends)(copy.start)

    def receive(s, r):
        for sends, receives, copy in messages(s, r):
            pl.when(receives)(copy.wait_recv)
            pl.when(sends)(copy.wait_send)

        @pl.when(has_down)
        def _():
            for c in range(3):
                E[r, c, 0, own_y, :] = xlo[s, r, c]
            if s == 0:
                H[r, 1, 0, own_y, :] = xlo_h[r, 0]
                H[r, 2, 0, own_y, :] = xlo_h[r, 1]

        @pl.when(has_up)
        def _():
            E[r, 1, X + 1, own_y, :] = xhi[s, r, 0]
            E[r, 2, X + 1, own_y, :] = xhi[s, r, 1]

        @pl.when(has_right)
        def _():
            for p in range(X):
                E[r, 0, p + 1, pl.ds(PAD + Y, 1), :] = r_left[s, r, 0, pl.ds(p, 1), :]
                E[r, 2, p + 1, pl.ds(PAD + Y, 1), :] = r_left[s, r, 1, pl.ds(p, 1), :]

        @pl.when(has_down & has_right)
        def _():
            E[r, 0, 0, pl.ds(PAD + Y, 1), :] = r_diag_b[s, r, pl.ds(0, 1), :]

    def next_z(value):
        lane = lax.broadcasted_iota(jnp.int32, value.shape, 1)
        return jnp.where(lane == Z - 1, 0.0, pltpu.roll(value, Z - 1, 1))

    def last_z(value):
        lane = lax.broadcasted_iota(jnp.int32, value.shape, 1)
        return jnp.where(lane == 0, 0.0, pltpu.roll(value, 1, 1))

    def update_h(s, r):
        above = pl.ds(PAD + 1, Y)
        for p in range(1, X + 1):
            ex, ey, ez = (E[r, c, p, own_y, :] for c in range(3))
            curl_x = (E[r, 2, p, above, :] - ez) - (next_z(ey) - ey)
            curl_y = (next_z(ex) - ex) - (E[r, 2, p + 1, own_y, :] - ez)
            curl_z = (E[r, 1, p + 1, own_y, :] - ey) - (E[r, 0, p, above, :] - ex)
            for c, curl in enumerate((curl_x, curl_y, curl_z)):
                H[r, c, p, own_y, :] = H[r, c, p, own_y, :] - time_step * curl

        @pl.when(has_down)
        def _():
            ex, ey, ez = (E[r, c, 0, own_y, :] for c in range(3))
            curl_y = (next_z(ex) - ex) - (E[r, 2, 1, own_y, :] - ez)
            curl_z = (E[r, 1, 1, own_y, :] - ey) - (E[r, 0, 0, above, :] - ex)
            H[r, 1, 0, own_y, :] = H[r, 1, 0, own_y, :] - time_step * curl_y
            H[r, 2, 0, own_y, :] = H[r, 2, 0, own_y, :] - time_step * curl_z

        @pl.when(has_left)
        def _():
            ex, ey, ez = (r_right[s, r, c] for c in range(3))
            if s == 0:
                hx, hz = r_right[s, r, 3], r_right[s, r, 4]
            else:
                hx, hz = h_row[r, 0], h_row[r, 1]
            plane = lax.broadcasted_iota(jnp.int32, (X, Z), 0)
            corner = jnp.broadcast_to(r_diag_a[s, r, pl.ds(PAD - 1, 1), :], (X, Z))
            corner = jnp.where(has_up, corner, 0.0)
            ey_up = jnp.where(plane == X - 1, corner, pltpu.roll(ey, X - 1, 0))
            hx = hx - time_step * ((s_left[s, r, 1] - ez) - (next_z(ey) - ey))
            hz = hz - time_step * ((ey_up - ey) - (s_left[s, r, 0] - ex))
            h_row[r, 0] = hx
            h_row[r, 1] = hz
            for p in range(X):
                H[r, 0, p + 1, pl.ds(PAD - 1, 1), :] = h_row[r, 0, pl.ds(p, 1), :]
                H[r, 2, p + 1, pl.ds(PAD - 1, 1), :] = h_row[r, 1, pl.ds(p, 1), :]

    def update_e(r):
        below = pl.ds(PAD - 1, Y)
        for p in range(1, X + 1):
            hx, hy, hz = (H[r, c, p, own_y, :] for c in range(3))
            curl_x = (hz - H[r, 2, p, below, :]) - (hy - last_z(hy))
            curl_y = (hx - last_z(hx)) - (hz - H[r, 2, p - 1, own_y, :])
            curl_z = (hy - H[r, 1, p - 1, own_y, :]) - (hx - H[r, 0, p, below, :])
            k = coef[r, p - 1]
            for c, curl in enumerate((curl_x, curl_y, curl_z)):
                E[r, c, p, own_y, :] = E[r, c, p, own_y, :] + k * (curl - J[c, p - 1])

    @pl.loop(1, W)
    def _(d):
        tile_copy(d).start()

    loads[1].wait()
    loads[2].wait()

    @pl.loop(0, R)
    def _(r):
        send(0, r)


    loads[3].wait()
    loads[4].wait()

    @pl.loop(1, W)
    def _(d):
        tile_copy(d).wait()

    mine, following = jnp.int32(0), jnp.int32(0)
    for t in range(W):
        mine = jnp.where(slabs[t] == w, t, mine)
        following = jnp.where(slabs[t] == w + 1, t, following)
    low = refine_weights(2 * HZ, Z, 0, HZ - 1)
    high = refine_weights(2 * HZ, Z, HZ, HZ - 1)
    block = gathered[mine]
    unpacked[0] = exact_dot(block, low)
    unpacked[1] = exact_dot(block, high)
    unpacked[2] = exact_dot(gathered[following], low)
    depth = coarse.shape[1]
    for p in range(TR + 1):
        coarse[p, pl.ds(HY, depth - HY), :] = jnp.zeros((depth - HY, Z), jnp.float32)
    for p in range(TR):
        coarse[p, pl.ds(0, HY), :] = unpacked[p // half, pl.ds((p % half) * HY, HY), :]
    last = unpacked[(TR - 1) // half, pl.ds(((TR - 1) % half) * HY, HY), :]
    coarse[TR, pl.ds(0, HY), :] = jnp.where(has_up, unpacked[2, pl.ds(0, HY), :], last)
    for p in range(TR + 1):
        row_send[pl.ds(p, 1), :] = coarse[p, pl.ds(0, 1), :]
    row_copy = pltpu.make_async_remote_copy(
        src_ref=row_send,
        dst_ref=row_recv,
        send_sem=row_sems.at[0],
        recv_sem=row_sems.at[1],
        device_id=(w, n - 1),
        device_id_type=MESH,
    )
    pl.when(has_left)(row_copy.start)
    pl.when(has_right)(row_copy.wait_recv)
    pl.when(has_left)(row_copy.wait_send)
    for p in range(TR + 1):

        @pl.when(has_right)
        def _():
            coarse[p, pl.ds(HY, 1), :] = row_recv[pl.ds(p, 1), :]

        @pl.when(jnp.logical_not(has_right))
        def _():
            coarse[p, pl.ds(HY, 1), :] = coarse[p, pl.ds(HY - 1, 1), :]

    fine_j = lax.broadcasted_iota(jnp.int32, (Y, depth), 0)
    coarse_k = lax.broadcasted_iota(jnp.int32, (Y, depth), 1)
    along_y = _weights(coarse_k, fine_j, HY)
    for p in range(TR + 1):
        unpacked[p] = exact_dot(along_y, coarse[p])

    level0, level1 = levels[0], levels[1]
    global_y = n * Y + lax.broadcasted_iota(jnp.int32, (Y, Z), 0)
    global_z = lax.broadcasted_iota(jnp.int32, (Y, Z), 1)
    inside_yz = (
        (global_y >= box[2]) & (global_y < box[3]) & (global_z >= box[4]) & (global_z < box[5])
    )

    @pl.loop(0, TR)
    def _(c):
        here = unpacked[c]
        for odd in range(2):
            density = 0.5 * (here + unpacked[c + 1]) if odd else here
            x = 2 * c + odd
            global_x = w * X + x
            x_inside = (global_x >= box[0]) & (global_x < box[1])
            inside = inside_yz & jnp.broadcast_to(x_inside, (Y, Z))
            background = jnp.where(mask[x] == 1, level1, level0)
            for r, threshold in enumerate(thresholds):
                low_end = math.tanh(sharpness * threshold)
                scale = low_end + math.tanh(sharpness * (1.0 - threshold))
                numer = low_end + jnp.tanh(sharpness * (density - threshold))
                design = level0 + (numer / scale) * (level1 - level0)
                coef[r, x] = time_step / jnp.where(inside, design, background)

    def store(r):
        return (
            pltpu.make_async_copy(
                H.at[r, :, own_x, own_y, :], h_out.at[r], out_sem.at[0, r]
            ),
            pltpu.make_async_copy(
                E.at[r, :, own_x, own_y, :], e_out.at[r], out_sem.at[1, r]
            ),
        )

    for s in range(STEPS):

        @pl.loop(0, R)
        def _(r):
            receive(s, r)
            update_h(s, r)
            if s == STEPS - 1:
                store(r)[0].start()
            update_e(r)
            if s < STEPS - 1:
                send(s + 1, r)
            else:
                store(r)[1].start()

    @pl.loop(0, R)
    def _(r):
        store(r)[0].wait()
        store(r)[1].wait()


def body(
    electric,
    magnetic,
    current,
    density_tiles,
    tile_slabs,
    design_box,
    material_mask,
    material_levels,
):
    W = lax.axis_size("wide")
    N = lax.axis_size("narrow")
    R, _, X, Y, Z = electric.shape
    TR, HY, HZ = density_tiles.shape
    f32 = jnp.float32
    smem = pl.BlockSpec(memory_space=pltpu.SMEM)
    hbm = pl.BlockSpec(memory_space=pl.ANY)
    depth = -(-(HY + 1) // 8) * 8
    dma = pltpu.SemaphoreType.DMA
    state = pltpu.VMEM((R, 3, X + 2, Y + 2 * PAD, Z), f32)
    scratch = [
        state,
        state,
        pltpu.VMEM((3, X, Y, Z), f32),
        pltpu.VMEM((HY, TR, HZ), f32),
        pltpu.VMEM((X, Y, Z), jnp.int32),
        pltpu.VMEM((R, X, Y, Z), f32),
        pltpu.VMEM((W, TR // 2 * HY, 2 * HZ), f32),
        pltpu.VMEM((TR + 1, Y, Z), f32),
        pltpu.VMEM((TR + 1, depth, Z), f32),
        pltpu.VMEM((8, Z), f32),
        pltpu.VMEM((8, Z), f32),
        pltpu.VMEM((STEPS, R, 3, Y, Z), f32),
        pltpu.VMEM((R, 2, Y, Z), f32),
        pltpu.VMEM((STEPS, R, 2, Y, Z), f32),
        pltpu.VMEM((STEPS, R, 5, X, Z), f32),
        pltpu.VMEM((STEPS, R, 5, X, Z), f32),
        pltpu.VMEM((STEPS, R, 2, X, Z), f32),
        pltpu.VMEM((STEPS, R, 2, X, Z), f32),
        pltpu.VMEM((STEPS, R, PAD, Z), f32),
        pltpu.VMEM((STEPS, R, PAD, Z), f32),
        pltpu.VMEM((R, 2, X, Z), f32),
        dma((5,)),
        dma((2, R)),
        dma((STEPS, R, 7)),
        dma((STEPS, R, 7)),
        dma((W,)),
        dma((W,)),
        dma((2,)),
    ]
    out = pltpu.VMEM(electric.shape, f32)
    return pl.pallas_call(
        functools.partial(kernel, W, N),
        out_shape=(out, out),
        in_specs=[smem, smem, smem] + [hbm] * 5,
        out_specs=(pl.BlockSpec(memory_space=pltpu.VMEM),) * 2,
        scratch_shapes=scratch,
        compiler_params=pltpu.CompilerParams(
            collective_id=0, has_side_effects=True, vmem_limit_bytes=62914560
        ),
        name="window",
    )(
        tile_slabs,
        design_box,
        material_levels,
        electric,
        magnetic,
        current,
        jnp.transpose(density_tiles, (1, 0, 2)),
        material_mask,
    )


def solution(mesh):
    strip = P(None, None, "wide", "narrow", None)
    return jax.shard_map(
        body,
        mesh=mesh,
        in_specs=(
            strip,
            strip,
            P(None, "wide", "narrow", None),
            P("wide", "narrow", None),
            P(),
            P(),
            P("wide", "narrow", None),
            P(),
        ),
        out_specs=(strip, strip),
        check_vma=False,
    )
```

profile of v0, /device:TPU:0, one launch (start us, length us, event | category | flops | bytes accessed | tf_op | source)
XLA Modules:
  0.0 35.1 jit_solution(13760186720466060801)
XLA Ops:
  0.6 32.6 %window.1 = (f32[3,3,8,24,128]{4,3,2,1,0:T(8,128)S(1)}, f32[3,3,8,24,128]{4,3,2,1,0:T(8,128)S(1)}) custom-call(s32[16]{0:T(128)} %slabs.1, s32[6]{0:T(128)} %box.1, f32[2]{0:T(128)} %levels.1, f32[3,3,8,24,128]{4,3,2,1,0:T(8,128)} %e_in.1, f32[3,3,8,24,128]{4,3,2,1,0:T(8,128)} %h_in.1, f32[3,8,24,128]{3,2,1,0:T(8,128)} %j_in.1, f32[12,4,64]{2,1,0:T(4,128)} %bitcast.1, ...), custom_call_target="tpu_custom_call" | custom-call | tf_op jit(solution)/shard_map/window/pallas_call | solution.py:481
  33.3 0.9 %copy.12 = f32[3,3,8,24,128]{4,3,2,1,0:T(8,128)} copy(f32[3,3,8,24,128]{4,3,2,1,0:T(8,128)S(1)} %get-tuple-element.2) | data formatting | bytes 1769472
  34.2 0.9 %copy.13 = f32[3,3,8,24,128]{4,3,2,1,0:T(8,128)} copy(f32[3,3,8,24,128]{4,3,2,1,0:T(8,128)S(1)} %get-tuple-element.3) | data formatting | bytes 1769472
where the time goes:
time: 35.2 us; the launch traced here: 35.1 us
  Pallas kernels  32.6 us (93%)
  local copies, waits for them, and re-layouts  1.83 us (5%)
  between operations  0.64 us (2%)
    pallas_call x1, Pallas kernels, body(): pl.pallas_call(functools.partial(kernel, W, N), out_shape=(out, out), in_...  32.6 us
    unnamed x2, local copies, waits for them, and re-layouts  1.83 us

commit v1 on v0

--- a/solution.py
+++ b/solution.py
@@ -15,7 +15,7 @@
 
 PAD = 8
 MESH = pl.DeviceIdType.MESH
-UP, DOWN, RIGHT, LEFT, DIAG_A, DIAG_B, UP_H = range(7)
+UP, DOWN, RIGHT, LEFT, DIAG_A, DIAG_B = range(6)
 
 
 def refine_weights(rows, columns, offset, cells):
@@ -39,18 +39,19 @@
 def kernel(
     W,
     N,
-    slabs,
-    box,
-    levels,
+    slabs_in,
+    box_in,
+    levels_in,
     e_in,
     h_in,
     j_in,
     tiles_in,
     mask_in,
-    e_out,
-    h_out,
     E,
     H,
+    slabs,
+    box,
+    levels,
     J,
     tile,
     mask,
@@ -60,8 +61,8 @@
     coarse,
     row_send,
     row_recv,
+    s_up,
     xlo,
-    xlo_h,
     xhi,
     s_right,
     r_right,
@@ -71,17 +72,14 @@
     r_diag_b,
     h_row,
     load_sem,
-    out_sem,
     send_sem,
     recv_sem,
-    tile_send,
-    tile_recv,
+    tile_sems,
     row_sems,
 ):
     w = lax.axis_index("wide")
     n = lax.axis_index("narrow")
-    R, _, X, _, Z = e_out.shape
-    Y = e_out.shape[3]
+    R, _, X, Y, Z = e_in.shape
     HY, TR, HZ = tiles_in.shape
     own_x = pl.ds(1, X)
     own_y = pl.ds(PAD, Y)
@@ -92,6 +90,9 @@
         pltpu.make_async_copy(h_in, H.at[:, :, own_x, own_y, :], load_sem.at[2]),
         pltpu.make_async_copy(j_in, J, load_sem.at[3]),
         pltpu.make_async_copy(mask_in, mask, load_sem.at[4]),
+        pltpu.make_async_copy(slabs_in, slabs, load_sem.at[5]),
+        pltpu.make_async_copy(box_in, box, load_sem.at[6]),
+        pltpu.make_async_copy(levels_in, levels, load_sem.at[7]),
     ]
     for load in loads:
         load.start()
@@ -129,7 +130,6 @@
     @pl.loop(0, R)
     def _(r):
         for c in range(3):
-            E[r, c, 0] = zero_plane
             E[r, c, X + 1] = zero_plane
             H[r, c, 0] = zero_plane
             for p in range(1, X + 1):
@@ -150,107 +150,103 @@
         return pltpu.make_async_remote_copy(
             src_ref=gathered.at[w],
             dst_ref=gathered.at[w],
-            send_sem=tile_send.at[d],
-            recv_sem=tile_recv.at[d],
+            send_sem=tile_sems.at[0],
+            recv_sem=tile_sems.at[1],
             device_id=(lax.rem(w + d, W), n),
             device_id_type=MESH,
         )
 
     def messages(s, r):
+        b = s % 2
+
         def copy(kind, src, dst, to_w, to_n):
             return pltpu.make_async_remote_copy(
                 src_ref=src,
                 dst_ref=dst,
-                send_sem=send_sem.at[s, r, kind],
-                recv_sem=recv_sem.at[s, r, kind],
+                send_sem=send_sem.at[r, kind],
+                recv_sem=recv_sem.at[b, r, kind],
                 device_id=(to_w, to_n),
                 device_id_type=MESH,
             )
 
         rows = 5 if s == 0 else 3
-        found = [
-            (has_up, has_down, copy(UP, E.at[r, :, X, own_y, :], xlo.at[s, r], w + 1, n)),
+        return [
+            (has_up, has_down, copy(UP, s_up.at[b, r], xlo.at[b, r], w + 1, n)),
             (
                 has_down,
                 has_up,
-                copy(DOWN, E.at[r, pl.ds(1, 2), 1, own_y, :], xhi.at[s, r], w - 1, n),
+                copy(DOWN, E.at[r, pl.ds(1, 2), 1, own_y, :], xhi.at[b, r], w - 1, n),
             ),
             (
                 has_right,
                 has_left,
                 copy(
                     RIGHT,
-                    s_right.at[s, r, pl.ds(0, rows)],
-                    r_right.at[s, r, pl.ds(0, rows)],
+                    s_right.at[b, r, pl.ds(0, rows)],
+                    r_right.at[b, r, pl.ds(0, rows)],
                     w,
                     n + 1,
                 ),
             ),
-            (has_left, has_right, copy(LEFT, s_left.at[s, r], r_left.at[s, r], w, n - 1)),
+            (has_left, has_right, copy(LEFT, s_left.at[b, r], r_left.at[b, r], w, n - 1)),
             (
                 has_down & has_right,
                 has_up & has_left,
                 copy(
-                    DIAG_A, E.at[r, 1, 1, pl.ds(Y, PAD), :], r_diag_a.at[s, r], w - 1, n + 1
+                    DIAG_A, E.at[r, 1, 1, pl.ds(Y, PAD), :], r_diag_a.at[b, r], w - 1, n + 1
                 ),
             ),
             (
                 has_up & has_left,
                 has_down & has_right,
                 copy(
-                    DIAG_B, E.at[r, 0, X, pl.ds(PAD, PAD), :], r_diag_b.at[s, r], w + 1, n - 1
+                    DIAG_B, E.at[r, 0, X, pl.ds(PAD, PAD), :], r_diag_b.at[b, r], w + 1, n - 1
                 ),
             ),
         ]
-        if s == 0:
-            found.append(
-                (
-                    has_up,
-                    has_down,
-                    copy(UP_H, H.at[r, pl.ds(1, 2), X, own_y, :], xlo_h.at[r], w + 1, n),
-                )
-            )
-        return found
+
+    last_row = lax.broadcasted_iota(jnp.int32, (Y, Z), 0) == Y - 1
 
     def send(s, r):
+        b = s % 2
+        ex, ey, ez = (E[r, c, X, own_y, :] for c in range(3))
+        beyond = jnp.where(last_row, 0.0, E[r, 0, X, pl.ds(PAD + 1, Y), :])
+        s_up[b, r, 0] = H[r, 1, X, own_y, :] - time_step * ((next_z(ex) - ex) + ez)
+        s_up[b, r, 1] = H[r, 2, X, own_y, :] + time_step * ((beyond - ex) + ey)
         for p in range(X):
             for c in range(3):
-                s_right[s, r, c, pl.ds(p, 1), :] = E[r, c, p + 1, pl.ds(PAD + Y - 1, 1), :]
+                s_right[b, r, c, pl.ds(p, 1), :] = E[r, c, p + 1, pl.ds(PAD + Y - 1, 1), :]
             if s == 0:
-                s_right[s, r, 3, pl.ds(p, 1), :] = H[r, 0, p + 1, pl.ds(PAD + Y - 1, 1), :]
-                s_right[s, r, 4, pl.ds(p, 1), :] = H[r, 2, p + 1, pl.ds(PAD + Y - 1, 1), :]
-            s_left[s, r, 0, pl.ds(p, 1), :] = E[r, 0, p + 1, pl.ds(PAD, 1), :]
-            s_left[s, r, 1, pl.ds(p, 1), :] = E[r, 2, p + 1, pl.ds(PAD, 1), :]
+                s_right[b, r, 3, pl.ds(p, 1), :] = H[r, 0, p + 1, pl.ds(PAD + Y - 1, 1), :]
+                s_right[b, r, 4, pl.ds(p, 1), :] = H[r, 2, p + 1, pl.ds(PAD + Y - 1, 1), :]
+            s_left[b, r, 0, pl.ds(p, 1), :] = E[r, 0, p + 1, pl.ds(PAD, 1), :]
+            s_left[b, r, 1, pl.ds(p, 1), :] = E[r, 2, p + 1, pl.ds(PAD, 1), :]
         for sends, _, copy in messages(s, r):
             pl.when(sends)(copy.start)
 
     def receive(s, r):
+        b = s % 2
         for sends, receives, copy in messages(s, r):
             pl.when(receives)(copy.wait_recv)
             pl.when(sends)(copy.wait_send)
 
         @pl.when(has_down)
         def _():
-            for c in range(3):
-                E[r, c, 0, own_y, :] = xlo[s, r, c]
-            if s == 0:
-                H[r, 1, 0, own_y, :] = xlo_h[r, 0]
-                H[r, 2, 0, own_y, :] = xlo_h[r, 1]
+            H[r, 1, 0, own_y, :] = xlo[b, r, 0] + time_step * E[r, 2, 1, own_y, :]
+            corner = jnp.broadcast_to(r_diag_b[b, r, pl.ds(0, 1), :], (Y, Z))
+            corner = jnp.where(last_row & jnp.broadcast_to(has_right, (Y, Z)), corner, 0.0)
+            H[r, 2, 0, own_y, :] = xlo[b, r, 1] + time_step * (corner - E[r, 1, 1, own_y, :])
 
         @pl.when(has_up)
         def _():
-            E[r, 1, X + 1, own_y, :] = xhi[s, r, 0]
-            E[r, 2, X + 1, own_y, :] = xhi[s, r, 1]
+            E[r, 1, X + 1, own_y, :] = xhi[b, r, 0]
+            E[r, 2, X + 1, own_y, :] = xhi[b, r, 1]
 
         @pl.when(has_right)
         def _():
             for p in range(X):
-                E[r, 0, p + 1, pl.ds(PAD + Y, 1), :] = r_left[s, r, 0, pl.ds(p, 1), :]
-                E[r, 2, p + 1, pl.ds(PAD + Y, 1), :] = r_left[s, r, 1, pl.ds(p, 1), :]
-
-        @pl.when(has_down & has_right)
-        def _():
-            E[r, 0, 0, pl.ds(PAD + Y, 1), :] = r_diag_b[s, r, pl.ds(0, 1), :]
+                E[r, 0, p + 1, pl.ds(PAD + Y, 1), :] = r_left[b, r, 0, pl.ds(p, 1), :]
+                E[r, 2, p + 1, pl.ds(PAD + Y, 1), :] = r_left[b, r, 1, pl.ds(p, 1), :]
 
     def next_z(value):
         lane = lax.broadcasted_iota(jnp.int32, value.shape, 1)
@@ -261,6 +257,7 @@
         return jnp.where(lane == 0, 0.0, pltpu.roll(value, 1, 1))
 
     def update_h(s, r):
+        b = s % 2
         above = pl.ds(PAD + 1, Y)
         for p in range(1, X + 1):
             ex, ey, ez = (E[r, c, p, own_y, :] for c in range(3))
@@ -270,27 +267,19 @@
             for c, curl in enumerate((curl_x, curl_y, curl_z)):
                 H[r, c, p, own_y, :] = H[r, c, p, own_y, :] - time_step * curl
 
-        @pl.when(has_down)
-        def _():
-            ex, ey, ez = (E[r, c, 0, own_y, :] for c in range(3))
-            curl_y = (next_z(ex) - ex) - (E[r, 2, 1, own_y, :] - ez)
-            curl_z = (E[r, 1, 1, own_y, :] - ey) - (E[r, 0, 0, above, :] - ex)
-            H[r, 1, 0, own_y, :] = H[r, 1, 0, own_y, :] - time_step * curl_y
-            H[r, 2, 0, own_y, :] = H[r, 2, 0, own_y, :] - time_step * curl_z
-
         @pl.when(has_left)
         def _():
-            ex, ey, ez = (r_right[s, r, c] for c in range(3))
+            ex, ey, ez = (r_right[b, r, c] for c in range(3))
             if s == 0:
-                hx, hz = r_right[s, r, 3], r_right[s, r, 4]
+                hx, hz = r_right[b, r, 3], r_right[b, r, 4]
             else:
                 hx, hz = h_row[r, 0], h_row[r, 1]
             plane = lax.broadcasted_iota(jnp.int32, (X, Z), 0)
-            corner = jnp.broadcast_to(r_diag_a[s, r, pl.ds(PAD - 1, 1), :], (X, Z))
+            corner = jnp.broadcast_to(r_diag_a[b, r, pl.ds(PAD - 1, 1), :], (X, Z))
             corner = jnp.where(has_up, corner, 0.0)
             ey_up = jnp.where(plane == X - 1, corner, pltpu.roll(ey, X - 1, 0))
-            hx = hx - time_step * ((s_left[s, r, 1] - ez) - (next_z(ey) - ey))
-            hz = hz - time_step * ((ey_up - ey) - (s_left[s, r, 0] - ex))
+            hx = hx - time_step * ((s_left[b, r, 1] - ez) - (next_z(ey) - ey))
+            hz = hz - time_step * ((ey_up - ey) - (s_left[b, r, 0] - ex))
             h_row[r, 0] = hx
             h_row[r, 1] = hz
             for p in range(X):
@@ -323,9 +312,11 @@
     loads[3].wait()
     loads[4].wait()
 
-    @pl.loop(1, W)
-    def _(d):
-        tile_copy(d).wait()
+    others_tiles = gathered.at[pl.ds(0, W - 1)]
+    for i in range(2):
+        pltpu.make_async_copy(others_tiles, others_tiles, tile_sems.at[i]).wait()
+    for load in loads[5:]:
+        load.wait()
 
     mine, following = jnp.int32(0), jnp.int32(0)
     for t in range(W):
@@ -397,34 +388,28 @@
                 design = level0 + (numer / scale) * (level1 - level0)
                 coef[r, x] = time_step / jnp.where(inside, design, background)
 
-    def store(r):
-        return (
-            pltpu.make_async_copy(
-                H.at[r, :, own_x, own_y, :], h_out.at[r], out_sem.at[0, r]
-            ),
-            pltpu.make_async_copy(
-                E.at[r, :, own_x, own_y, :], e_out.at[r], out_sem.at[1, r]
-            ),
-        )
-
     for s in range(STEPS):
 
         @pl.loop(0, R)
         def _(r):
             receive(s, r)
             update_h(s, r)
-            if s == STEPS - 1:
-                store(r)[0].start()
             update_e(r)
             if s < STEPS - 1:
                 send(s + 1, r)
-            else:
-                store(r)[1].start()
-
-    @pl.loop(0, R)
-    def _(r):
-        store(r)[0].wait()
-        store(r)[1].wait()
+
+
+def write_out(e, h, e_out, h_out, sems):
+    X, Y = e_out.shape[2:4]
+    own = (slice(None), slice(None), pl.ds(1, X), pl.ds(PAD, Y), slice(None))
+    copies = [
+        pltpu.make_async_copy(e.at[own], e_out, sems.at[0]),
+        pltpu.make_async_copy(h.at[own], h_out, sems.at[1]),
+    ]
+    for copy in copies:
+        copy.start()
+    for copy in copies:
+        copy.wait()
 
 
 def body(
@@ -442,14 +427,14 @@
     R, _, X, Y, Z = electric.shape
     TR, HY, HZ = density_tiles.shape
     f32 = jnp.float32
-    smem = pl.BlockSpec(memory_space=pltpu.SMEM)
     hbm = pl.BlockSpec(memory_space=pl.ANY)
+    vmem = pl.BlockSpec(memory_space=pltpu.VMEM)
     depth = -(-(HY + 1) // 8) * 8
     dma = pltpu.SemaphoreType.DMA
-    state = pltpu.VMEM((R, 3, X + 2, Y + 2 * PAD, Z), f32)
     scratch = [
-        state,
-        state,
+        pltpu.SMEM(tile_slabs.shape, jnp.int32),
+        pltpu.SMEM(design_box.shape, jnp.int32),
+        pltpu.SMEM(material_levels.shape, f32),
         pltpu.VMEM((3, X, Y, Z), f32),
         pltpu.VMEM((HY, TR, HZ), f32),
         pltpu.VMEM((X, Y, Z), jnp.int32),
@@ -459,33 +444,31 @@
         pltpu.VMEM((TR + 1, depth, Z), f32),
         pltpu.VMEM((8, Z), f32),
         pltpu.VMEM((8, Z), f32),
-        pltpu.VMEM((STEPS, R, 3, Y, Z), f32),
-        pltpu.VMEM((R, 2, Y, Z), f32),
-        pltpu.VMEM((STEPS, R, 2, Y, Z), f32),
-        pltpu.VMEM((STEPS, R, 5, X, Z), f32),
-        pltpu.VMEM((STEPS, R, 5, X, Z), f32),
-        pltpu.VMEM((STEPS, R, 2, X, Z), f32),
-        pltpu.VMEM((STEPS, R, 2, X, Z), f32),
-        pltpu.VMEM((STEPS, R, PAD, Z), f32),
-        pltpu.VMEM((STEPS, R, PAD, Z), f32),
+        pltpu.VMEM((2, R, 2, Y, Z), f32),
+        pltpu.VMEM((2, R, 2, Y, Z), f32),
+        pltpu.VMEM((2, R, 2, Y, Z), f32),
+        pltpu.VMEM((2, R, 5, X, Z), f32),
+        pltpu.VMEM((2, R, 5, X, Z), f32),
+        pltpu.VMEM((2, R, 2, X, Z), f32),
+        pltpu.VMEM((2, R, 2, X, Z), f32),
+        pltpu.VMEM((2, R, PAD, Z), f32),
+        pltpu.VMEM((2, R, PAD, Z), f32),
         pltpu.VMEM((R, 2, X, Z), f32),
-        dma((5,)),
-        dma((2, R)),
-        dma((STEPS, R, 7)),
-        dma((STEPS, R, 7)),
-        dma((W,)),
-        dma((W,)),
+        dma((8,)),
+        dma((R, 6)),
+        dma((2, R, 6)),
+        dma((2,)),
         dma((2,)),
     ]
-    out = pltpu.VMEM(electric.shape, f32)
-    return pl.pallas_call(
+    state = pltpu.VMEM((R, 3, X + 2, Y + 2 * PAD, Z), f32)
+    e, h = pl.pallas_call(
         functools.partial(kernel, W, N),
-        out_shape=(out, out),
-        in_specs=[smem, smem, smem] + [hbm] * 5,
-        out_specs=(pl.BlockSpec(memory_space=pltpu.VMEM),) * 2,
+        out_shape=(state, state),
+        in_specs=[hbm] * 8,
+        out_specs=(vmem,) * 2,
         scratch_shapes=scratch,
         compiler_params=pltpu.CompilerParams(
-            collective_id=0, has_side_effects=True, vmem_limit_bytes=62914560
+            collective_id=0, has_side_effects=True, vmem_limit_bytes=56623104
         ),
         name="window",
     )(
@@ -498,6 +481,16 @@
         jnp.transpose(density_tiles, (1, 0, 2)),
         material_mask,
     )
+    out = jax.ShapeDtypeStruct(electric.shape, f32)
+    return pl.pallas_call(
+        write_out,
+        out_shape=(out, out),
+        in_specs=[vmem] * 2,
+        out_specs=(hbm,) * 2,
+        scratch_shapes=[dma((2,))],
+        compiler_params=pltpu.CompilerParams(vmem_limit_bytes=2**20),
+        name="write_out",
+    )(e, h)
 
 
 def solution(mesh):

time: 35.2 us -> 30.3 us (0.86)
  Pallas kernels: 32.6 us -> 29.5 us
  local copies, waits for them, and re-layouts: 1.83 us -> 0 us
    pallas_call x1 -> x2, Pallas kernels: 32.6 us -> 29.5 us  [the longest x1 28.3 us: body(): pl.pallas_call(functools.partial(kernel, W, N), out_shape=(state, state),...]
    unnamed x2 -> x0, local copies, waits for them, and re-layouts: 1.83 us -> none
where the time goes in v1:
time: 30.3 us; the launch traced here: 30.1 us
  Pallas kernels  29.5 us (97%)
  between operations  0.64 us (2%)
    pallas_call x1, Pallas kernels, body(): pl.pallas_call(functools.partial(kernel, W, N), out_shape=(state, state),...  28.3 us
    pallas_call x1, Pallas kernels, body(): pl.pallas_call(write_out, out_shape=(out, out), in_specs=[vmem] * 2, out_...  1.22 us

profile of v1, /device:TPU:0, one launch (start us, length us, event | category | flops | bytes accessed | tf_op | source)
XLA Modules:
  0.0 30.1 jit_solution(3102315129161230599)
XLA Ops:
  0.6 28.3 %window.1 = (f32[3,3,10,40,128]{4,3,2,1,0:T(8,128)S(1)}, f32[3,3,10,40,128]{4,3,2,1,0:T(8,128)S(1)}) custom-call(s32[16]{0:T(128)} %slabs_in.1, s32[6]{0:T(128)} %box_in.1, f32[2]{0:T(128)} %levels_in.1, f32[3,3,8,24,128]{4,3,2,1,0:T(8,128)} %e_in.1, f32[3,3,8,24,128]{4,3,2,1,0:T(8,128)} %h_in.1, f32[3,8,24,128]{3,2,1,0:T(8,128)} %j_in.1, ...), custom_call_target="tpu_custom_call" | custom-call | tf_op jit(solution)/shard_map/window/pallas_call | solution.py:464
  28.9 1.2 %write_out.1 = (f32[3,3,8,24,128]{4,3,2,1,0:T(8,128)}, f32[3,3,8,24,128]{4,3,2,1,0:T(8,128)}) custom-call(f32[3,3,10,40,128]{4,3,2,1,0:T(8,128)S(1)} %get-tuple-element.4.e, f32[3,3,10,40,128]{4,3,2,1,0:T(8,128)S(1)} %get-tuple-element.5.h), custom_call_target="tpu_custom_call" | custom-call | tf_op jit(solution)/shard_map/write_out/pallas_call | solution.py:485

commit v2 on v1

v2 whole, which is shorter than its diff:
```python
import functools
import math

import jax
import jax.numpy as jnp
from jax import lax
from jax.experimental import pallas as pl
from jax.experimental.pallas import tpu as pltpu
from jax.sharding import PartitionSpec as P

STEPS = 4
sharpness = 8.0
thresholds = (0.7, 0.5, 0.3)
time_step = 0.5

PAD = 8
MESH = pl.DeviceIdType.MESH
UP, DOWN, DIAG_A, DIAG_B, RIGHT, LEFT = range(6)


def refine_weights(rows, columns, offset, cells):
    k = lax.broadcasted_iota(jnp.int32, (rows, columns), 0) - offset
    j = lax.broadcasted_iota(jnp.int32, (rows, columns), 1)
    return _weights(k, j, cells)


def _weights(k, j, last):
    cell = j >> 1
    odd = (j & 1) == 1
    here = jnp.where(k == cell, jnp.where(odd, 0.5, 1.0), 0.0)
    above = jnp.where(odd & (k == jnp.minimum(cell + 1, last)), 0.5, 0.0)
    return here + above


def exact_dot(a, b):
    return jnp.dot(a, b, precision=lax.Precision.HIGHEST, preferred_element_type=jnp.float32)


def plane_size(devices):
    size = 1
    for divisor in range(1, devices + 1):
        if devices % divisor == 0 and divisor * divisor <= devices:
            size = divisor
    return size


def kernel(
    W,
    N,
    slabs_in,
    box_in,
    levels_in,
    e_in,
    h_in,
    j_in,
    tiles_in,
    mask_in,
    E,
    H,
    slabs,
    box,
    levels,
    J,
    tile,
    mask,
    coef,
    line,
    chosen,
    found,
    density,
    first_rows,
    s_up,
    xlo,
    xhi,
    s_right,
    r_right,
    s_left,
    r_left,
    r_diag_a,
    r_diag_b,
    h_row,
    load_sem,
    send_sem,
    recv_sem,
    tile_sems,
):
    w = lax.axis_index("wide")
    n = lax.axis_index("narrow")
    R, _, X, Y, Z = e_in.shape
    HY, TR, HZ = tiles_in.shape
    half = TR // 2
    packed = half * HY
    P_ = plane_size(W)
    L = W // P_
    g = lax.div(w, P_)
    j = lax.rem(w, P_)
    own_x = pl.ds(1, X)
    own_y = pl.ds(PAD, Y)

    loads = [
        pltpu.make_async_copy(tiles_in, tile, load_sem.at[0]),
        pltpu.make_async_copy(e_in, E.at[:, :, own_x, own_y, :], load_sem.at[1]),
        pltpu.make_async_copy(h_in, H.at[:, :, own_x, own_y, :], load_sem.at[2]),
        pltpu.make_async_copy(slabs_in, slabs, load_sem.at[3]),
        pltpu.make_async_copy(j_in, J, load_sem.at[4]),
        pltpu.make_async_copy(mask_in, mask, load_sem.at[5]),
        pltpu.make_async_copy(box_in, box, load_sem.at[6]),
        pltpu.make_async_copy(levels_in, levels, load_sem.at[7]),
    ]
    for load in loads:
        load.start()

    has_up = w < W - 1
    has_down = w > 0
    has_right = n < N - 1
    has_left = n > 0

    for l in range(L):
        line[l, pl.ds(packed, line.shape[1] - packed), :] = jnp.zeros(
            (line.shape[1] - packed, Z), jnp.float32
        )

    barrier = pltpu.get_barrier_semaphore()

    def greet(to_w, to_n):
        pl.semaphore_signal(barrier, inc=1, device_id=(to_w, to_n), device_id_type=MESH)

    def along_line(d):
        return lax.rem(g + d, L) * P_ + j

    def in_plane(d):
        return g * P_ + lax.rem(j + d, P_)

    expected = L - 1 + P_ - 1
    for d in range(1, L):
        greet(along_line(d), n)
    for d in range(1, P_):
        greet(in_plane(d), n)
    for there, to_w, to_n in (
        (has_up, w + 1, n),
        (has_down, w - 1, n),
        (has_down & has_right, w - 1, n + 1),
        (has_up & has_left, w + 1, n - 1),
    ):
        expected = expected + there.astype(jnp.int32)

        @pl.when(there)
        def _():
            greet(to_w, to_n)

    for there, to_n in ((has_right, n + 1), (has_left, n - 1)):
        expected = expected + L * there.astype(jnp.int32)

        @pl.when(there)
        def _():
            for d in range(L):
                greet(along_line(d), to_n)

    zero_plane = jnp.zeros((Y + 2 * PAD, Z), jnp.float32)
    zero_tile = jnp.zeros((PAD, Z), jnp.float32)

    @pl.loop(0, R)
    def _(r):
        for c in range(3):
            E[r, c, X + 1] = zero_plane
            H[r, c, 0] = zero_plane
            for p in range(1, X + 1):
                E[r, c, p, pl.ds(PAD + Y, PAD), :] = zero_tile
                H[r, c, p, pl.ds(0, PAD), :] = zero_tile

    rest = chosen.shape[1] - packed - HY
    for c in range(P_):
        chosen[c, pl.ds(packed + HY, rest), :] = jnp.zeros((rest, Z), jnp.float32)

    loads[0].wait()
    for p in range(half):
        rows = jnp.concatenate([tile[:, p, :], tile[:, p + half, :]], axis=-1)
        line[g, pl.ds(p * HY, HY), :] = rows
        first_rows[pl.ds(p, 1), :] = rows[0:1]

    pl.semaphore_wait(barrier, expected)

    def tile_copy(src, dst, k, to_w, to_n):
        return pltpu.make_async_remote_copy(
            src_ref=src,
            dst_ref=dst,
            send_sem=tile_sems.at[2 * k],
            recv_sem=tile_sems.at[2 * k + 1],
            device_id=(to_w, to_n),
            device_id_type=MESH,
        )

    for d in range(1, L):
        mine = line.at[g, pl.ds(0, packed)]
        tile_copy(mine, mine, 0, along_line(d), n).start()

    @pl.when(has_left)
    def _():
        for d in range(L):
            tile_copy(
                first_rows.at[pl.ds(0, half)],
                line.at[g, pl.ds(packed, half)],
                1,
                along_line(d),
                n - 1,
            ).start()

    def all_bytes(ref, k):
        return pltpu.make_async_copy(ref, ref, tile_sems.at[k])

    def copies(s, r):
        b = s % 2

        def copy(kind, src, dst, to_w, to_n):
            return pltpu.make_async_remote_copy(
                src_ref=src,
                dst_ref=dst,
                send_sem=send_sem.at[r, kind],
                recv_sem=recv_sem.at[b, r, kind],
                device_id=(to_w, to_n),
                device_id_type=MESH,
            )

        rows = 5 if s == 0 else 3
        wide = [
            (
                has_down & has_right,
                has_up & has_left,
                copy(
                    DIAG_A,
                    E.at[r, 1, 1, pl.ds(PAD + Y - 1, 1), :],
                    r_diag_a.at[b, r],
                    w - 1,
                    n + 1,
                ),
            ),
            (
                has_up & has_left,
                has_down & has_right,
                copy(
                    DIAG_B, E.at[r, 0, X, pl.ds(PAD, 1), :], r_diag_b.at[b, r], w + 1, n - 1
                ),
            ),
            (has_up, has_down, copy(UP, s_up.at[b, r], xlo.at[b, r], w + 1, n)),
            (
                has_down,
                has_up,
                copy(DOWN, E.at[r, pl.ds(1, 2), 1, own_y, :], xhi.at[b, r], w - 1, n),
            ),
        ]
        narrow = [
            (
                has_right,
                has_left,
                copy(
                    RIGHT,
                    s_right.at[b, r, pl.ds(0, rows)],
                    r_right.at[b, r, pl.ds(0, rows)],
                    w,
                    n + 1,
                ),
            ),
            (has_left, has_right, copy(LEFT, s_left.at[b, r], r_left.at[b, r], w, n - 1)),
        ]
        return wide, narrow

    def start(messages):
        for sends, _, copy in messages:
            pl.when(sends)(copy.start)

    def finish(messages):
        for sends, receives, copy in messages:
            pl.when(receives)(copy.wait_recv)
            pl.when(sends)(copy.wait_send)

    last_row = lax.broadcasted_iota(jnp.int32, (Y, Z), 0) == Y - 1

    def next_z(value):
        lane = lax.broadcasted_iota(jnp.int32, value.shape, 1)
        return jnp.where(lane == Z - 1, 0.0, pltpu.roll(value, Z - 1, 1))

    def last_z(value):
        lane = lax.broadcasted_iota(jnp.int32, value.shape, 1)
        return jnp.where(lane == 0, 0.0, pltpu.roll(value, 1, 1))

    def send_wide(s, r):
        b = s % 2
        ex, ey, ez = (E[r, c, X, own_y, :] for c in range(3))
        beyond = jnp.where(last_row, 0.0, E[r, 0, X, pl.ds(PAD + 1, Y), :])
        s_up[b, r, 0] = H[r, 1, X, own_y, :] - time_step * ((next_z(ex) - ex) + ez)
        s_up[b, r, 1] = H[r, 2, X, own_y, :] + time_step * ((beyond - ex) + ey)
        diag_a, diag_b, up, down = copies(s, r)[0]
        even = lax.rem(w, 2) == 0

        @pl.when(even)
        def _():
            start([diag_a, down, diag_b, up])

        @pl.when(jnp.logical_not(even))
        def _():
            start([diag_b, up, diag_a, down])

    def send_narrow(s, r):
        b = s % 2
        for p in range(X):
            for c in range(3):
                s_right[b, r, c, pl.ds(p, 1), :] = E[r, c, p + 1, pl.ds(PAD + Y - 1, 1), :]
            if s == 0:
                s_right[b, r, 3, pl.ds(p, 1), :] = H[r, 0, p + 1, pl.ds(PAD + Y - 1, 1), :]
                s_right[b, r, 4, pl.ds(p, 1), :] = H[r, 2, p + 1, pl.ds(PAD + Y - 1, 1), :]
            s_left[b, r, 0, pl.ds(p, 1), :] = E[r, 0, p + 1, pl.ds(PAD, 1), :]
            s_left[b, r, 1, pl.ds(p, 1), :] = E[r, 2, p + 1, pl.ds(PAD, 1), :]
        start(copies(s, r)[1])

    def receive_narrow(s, r):
        b = s % 2
        finish(copies(s, r)[1])

        @pl.when(has_right)
        def _():
            for p in range(X):
                E[r, 0, p + 1, pl.ds(PAD + Y, 1), :] = r_left[b, r, 0, pl.ds(p, 1), :]
                E[r, 2, p + 1, pl.ds(PAD + Y, 1), :] = r_left[b, r, 1, pl.ds(p, 1), :]

        @pl.when(has_left)
        def _():
            ex, ey, ez = (r_right[b, r, c] for c in range(3))
            if s == 0:
                hx, hz = r_right[b, r, 3], r_right[b, r, 4]
            else:
                hx, hz = h_row[r, 0], h_row[r, 1]
            plane = lax.broadcasted_iota(jnp.int32, (X, Z), 0)
            ey_up = jnp.where(plane == X - 1, 0.0, pltpu.roll(ey, X - 1, 0))
            h_row[r, 0] = hx - time_step * ((s_left[b, r, 1] - ez) - (next_z(ey) - ey))
            h_row[r, 1] = hz - time_step * ((ey_up - ey) - (s_left[b, r, 0] - ex))
            for p in range(X):
                H[r, 0, p + 1, pl.ds(PAD - 1, 1), :] = h_row[r, 0, pl.ds(p, 1), :]
                H[r, 2, p + 1, pl.ds(PAD - 1, 1), :] = h_row[r, 1, pl.ds(p, 1), :]

    def receive_wide(s, r):
        b = s % 2
        finish(copies(s, r)[0])

        @pl.when(has_down)
        def _():
            H[r, 1, 0, own_y, :] = xlo[b, r, 0] + time_step * E[r, 2, 1, own_y, :]
            corner = jnp.broadcast_to(r_diag_b[b, r], (Y, Z))
            corner = jnp.where(last_row & jnp.broadcast_to(has_right, (Y, Z)), corner, 0.0)
            H[r, 2, 0, own_y, :] = xlo[b, r, 1] + time_step * (corner - E[r, 1, 1, own_y, :])

        @pl.when(has_up)
        def _():
            E[r, 1, X + 1, own_y, :] = xhi[b, r, 0]
            E[r, 2, X + 1, own_y, :] = xhi[b, r, 1]

        @pl.when(has_up & has_left)
        def _():
            edge = h_row[r, 1, pl.ds(X - 1, 1), :]
            edge = edge - time_step * r_diag_a[b, r]
            h_row[r, 1, pl.ds(X - 1, 1), :] = edge
            H[r, 2, X, pl.ds(PAD - 1, 1), :] = edge

    def update_h(r, planes):
        above = pl.ds(PAD + 1, Y)
        for p in planes:
            ex, ey, ez = (E[r, c, p, own_y, :] for c in range(3))
            curl_x = (E[r, 2, p, above, :] - ez) - (next_z(ey) - ey)
            curl_y = (next_z(ex) - ex) - (E[r, 2, p + 1, own_y, :] - ez)
            curl_z = (E[r, 1, p + 1, own_y, :] - ey) - (E[r, 0, p, above, :] - ex)
            for c, curl in enumerate((curl_x, curl_y, curl_z)):
                H[r, c, p, own_y, :] = H[r, c, p, own_y, :] - time_step * curl

    def update_e(r, planes):
        below = pl.ds(PAD - 1, Y)
        for p in planes:
            hx, hy, hz = (H[r, c, p, own_y, :] for c in range(3))
            curl_x = (hz - H[r, 2, p, below, :]) - (hy - last_z(hy))
            curl_y = (hx - last_z(hx)) - (hz - H[r, 2, p - 1, own_y, :])
            curl_z = (hy - H[r, 1, p - 1, own_y, :]) - (hx - H[r, 0, p, below, :])
            k = coef[r, p - 1]
            for c, curl in enumerate((curl_x, curl_y, curl_z)):
                E[r, c, p, own_y, :] = E[r, c, p, own_y, :] + k * (curl - J[c, p - 1])

    inner_h = range(1, X)
    inner_e = range(2, X)
    edges = (1, X)

    loads[1].wait()
    loads[2].wait()

    @pl.loop(0, R)
    def _(r):
        send_wide(0, r)

    @pl.loop(0, R)
    def _(r):
        send_narrow(0, r)

    for load in loads[3:]:
        load.wait()

    if L > 1:
        for k in range(2):
            all_bytes(line.at[pl.ds(0, L - 1), pl.ds(0, packed)], k).wait()
    for there, k in ((has_left, 2), (has_right, 3)):

        @pl.when(there)
        def _():
            all_bytes(line.at[:, pl.ds(packed, half)], k).wait()

    for c in range(P_):
        a, b = jnp.int32(0), jnp.int32(0)
        for l in range(L):
            slab = slabs[l * P_ + j]
            a = jnp.where(slab == g * P_ + c, l, a)
            b = jnp.where(slab == g * P_ + c + 1, l, b)
        chosen[c, pl.ds(0, packed), :] = line[a, pl.ds(0, packed), :]
        chosen[c, pl.ds(packed, HY), :] = line[b, pl.ds(0, HY), :]
        chosen[c, pl.ds(packed + HY, half), :] = line[a, pl.ds(packed, half), :]
        chosen[c, pl.ds(packed + HY + half, 1), :] = line[b, pl.ds(packed, 1), :]
    found[j] = chosen[j]
    for d in range(1, P_):
        tile_copy(
            chosen.at[lax.rem(j + d, P_)], found.at[j], 2, in_plane(d), n
        ).start()

    @pl.loop(0, R)
    def _(r):
        receive_narrow(0, r)
        update_h(r, inner_h)

    if P_ > 1:
        for k in range(4, 6):
            all_bytes(found.at[pl.ds(0, P_ - 1)], k).wait()

    mine, following = jnp.int32(0), jnp.int32(0)
    for t in range(W):
        mine = jnp.where(slabs[t] == w, t % P_, mine)
        following = jnp.where(slabs[t] == w + 1, t % P_, following)
    total = found.shape[1]
    row = lax.broadcasted_iota(jnp.int32, (total, Z), 0)
    of_mine = (row < packed) | ((row >= packed + HY) & (row < packed + HY + half))
    block = jnp.where(of_mine, found[mine], found[following])
    refined = [
        exact_dot(block, refine_weights(2 * HZ, Z, 0, HZ - 1)),
        exact_dot(block, refine_weights(2 * HZ, Z, HZ, HZ - 1)),
    ]
    fine = lax.broadcasted_iota(jnp.int32, (Y, total), 0)
    source = lax.broadcasted_iota(jnp.int32, (Y, total), 1)
    cell = fine >> 1
    odd = (fine & 1) == 1

    def along_y(base, right):
        right = jnp.where(has_right, right, base + HY - 1)
        here = jnp.where(source == base + cell, jnp.where(odd, 0.5, 1.0), 0.0)
        next_cell = jnp.where(cell == HY - 1, right, base + cell + 1)
        return here + jnp.where(odd & (source == next_cell), 0.5, 0.0)

    weights = [along_y(p * HY, packed + HY + p) for p in range(half)]
    for p in range(TR):
        density[p] = exact_dot(weights[p % half], refined[p // half])
    beyond_last = exact_dot(along_y(packed, packed + HY + half), refined[0])
    density[TR] = jnp.where(has_up, beyond_last, density[TR - 1])

    level0, level1 = levels[0], levels[1]
    global_y = n * Y + lax.broadcasted_iota(jnp.int32, (Y, Z), 0)
    global_z = lax.broadcasted_iota(jnp.int32, (Y, Z), 1)
    inside_yz = (
        (global_y >= box[2]) & (global_y < box[3]) & (global_z >= box[4]) & (global_z < box[5])
    )

    @pl.loop(0, TR)
    def _(c):
        here = density[c]
        for odd_plane in range(2):
            value = 0.5 * (here + density[c + 1]) if odd_plane else here
            x = 2 * c + odd_plane
            global_x = w * X + x
            x_inside = (global_x >= box[0]) & (global_x < box[1])
            inside = inside_yz & jnp.broadcast_to(x_inside, (Y, Z))
            background = jnp.where(mask[x] == 1, level1, level0)
            for r, threshold in enumerate(thresholds):
                low_end = math.tanh(sharpness * threshold)
                scale = low_end + math.tanh(sharpness * (1.0 - threshold))
                numer = low_end + jnp.tanh(sharpness * (value - threshold))
                design = level0 + (numer / scale) * (level1 - level0)
                coef[r, x] = time_step / jnp.where(inside, design, background)

    for s in range(STEPS):
        if s > 0:

            @pl.loop(0, R)
            def _(r):
                receive_narrow(s, r)
                update_h(r, inner_h)
                update_e(r, inner_e)

        @pl.loop(0, R)
        def _(r):
            receive_wide(s, r)
            update_h(r, (X,))
            update_e(r, edges)
            if s < STEPS - 1:
                send_wide(s + 1, r)
                if s > 0:
                    send_narrow(s + 1, r)

        if s == 0:

            @pl.loop(0, R)
            def _(r):
                update_e(r, inner_e)
                if STEPS > 1:
                    send_narrow(1, r)


def write_out(e, h, e_out, h_out, sems):
    X, Y = e_out.shape[2:4]
    own = (slice(None), slice(None), pl.ds(1, X), pl.ds(PAD, Y), slice(None))
    copies = [
        pltpu.make_async_copy(e.at[own], e_out, sems.at[0]),
        pltpu.make_async_copy(h.at[own], h_out, sems.at[1]),
    ]
    for copy in copies:
        copy.start()
    for copy in copies:
        copy.wait()


def body(
    electric,
    magnetic,
    current,
    density_tiles,
    tile_slabs,
    design_box,
    material_mask,
    material_levels,
):
    W = lax.axis_size("wide")
    N = lax.axis_size("narrow")
    R, _, X, Y, Z = electric.shape
    TR, HY, HZ = density_tiles.shape
    f32 = jnp.float32
    hbm = pl.BlockSpec(memory_space=pl.ANY)
    vmem = pl.BlockSpec(memory_space=pltpu.VMEM)
    P_ = plane_size(W)
    L = W // P_
    half = TR // 2
    packed = half * HY
    total = -(-(packed + HY + half + 1) // 8) * 8
    dma = pltpu.SemaphoreType.DMA
    scratch = [
        pltpu.SMEM(tile_slabs.shape, jnp.int32),
        pltpu.SMEM(design_box.shape, jnp.int32),
        pltpu.SMEM(material_levels.shape, f32),
        pltpu.VMEM((3, X, Y, Z), f32),
        pltpu.VMEM((HY, TR, HZ), f32),
        pltpu.VMEM((X, Y, Z), jnp.int32),
        pltpu.VMEM((R, X, Y, Z), f32),
        pltpu.VMEM((L, -(-(packed + half) // 8) * 8, Z), f32),
        pltpu.VMEM((P_, total, Z), f32),
        pltpu.VMEM((P_, total, Z), f32),
        pltpu.VMEM((TR + 1, Y, Z), f32),
        pltpu.VMEM((8, Z), f32),
        pltpu.VMEM((2, R, 2, Y, Z), f32),
        pltpu.VMEM((2, R, 2, Y, Z), f32),
        pltpu.VMEM((2, R, 2, Y, Z), f32),
        pltpu.VMEM((2, R, 5, X, Z), f32),
        pltpu.VMEM((2, R, 5, X, Z), f32),
        pltpu.VMEM((2, R, 2, X, Z), f32),
        pltpu.VMEM((2, R, 2, X, Z), f32),
        pltpu.VMEM((2, R, 1, Z), f32),
        pltpu.VMEM((2, R, 1, Z), f32),
        pltpu.VMEM((R, 2, X, Z), f32),
        dma((8,)),
        dma((R, 6)),
        dma((2, R, 6)),
        dma((6,)),
    ]
    state = pltpu.VMEM((R, 3, X + 2, Y + 2 * PAD, Z), f32)
    e, h = pl.pallas_call(
        functools.partial(kernel, W, N),
        out_shape=(state, state),
        in_specs=[hbm] * 8,
        out_specs=(vmem,) * 2,
        scratch_shapes=scratch,
        compiler_params=pltpu.CompilerParams(
            collective_id=0, has_side_effects=True, vmem_limit_bytes=56623104
        ),
        name="window",
    )(
        tile_slabs,
        design_box,
        material_levels,
        electric,
        magnetic,
        current,
        jnp.transpose(density_tiles, (1, 0, 2)),
        material_mask,
    )
    out = jax.ShapeDtypeStruct(electric.shape, f32)
    return pl.pallas_call(
        write_out,
        out_shape=(out, out),
        in_specs=[vmem] * 2,
        out_specs=(hbm,) * 2,
        scratch_shapes=[dma((2,))],
        compiler_params=pltpu.CompilerParams(vmem_limit_bytes=2**20),
        name="write_out",
    )(e, h)


def solution(mesh):
    strip = P(None, None, "wide", "narrow", None)
    return jax.shard_map(
        body,
        mesh=mesh,
        in_specs=(
            strip,
            strip,
            P(None, "wide", "narrow", None),
            P("wide", "narrow", None),
            P(),
            P(),
            P("wide", "narrow", None),
            P(),
        ),
        out_specs=(strip, strip),
        check_vma=False,
    )
```

time: 30.3 us -> 28.4 us (0.937)
  Pallas kernels: 29.5 us -> 27.6 us
    pallas_call x1, Pallas kernels: 28.3 us -> 26.4 us  [body(): pl.pallas_call(functools.partial(kernel, W, N), out_shape=(state, state),...]
where the time goes in v2:
time: 28.4 us; the launch traced here: 28.3 us
  Pallas kernels  27.6 us (97%)
  between operations  0.64 us (2%)
    pallas_call x1, Pallas kernels, body(): pl.pallas_call(functools.partial(kernel, W, N), out_shape=(state, state),...  26.4 us
    pallas_call x1, Pallas kernels, body(): pl.pallas_call(write_out, out_shape=(out, out), in_specs=[vmem] * 2, out_...  1.22 us

profile of v2, /device:TPU:0, one launch (start us, length us, event | category | flops | bytes accessed | tf_op | source)
XLA Modules:
  0.0 28.3 jit_solution(1505537604637063112)
XLA Ops:
  0.6 26.4 %window.1 = (f32[3,3,10,40,128]{4,3,2,1,0:T(8,128)S(1)}, f32[3,3,10,40,128]{4,3,2,1,0:T(8,128)S(1)}) custom-call(s32[16]{0:T(128)} %slabs_in.1, s32[6]{0:T(128)} %box_in.1, f32[2]{0:T(128)} %levels_in.1, f32[3,3,8,24,128]{4,3,2,1,0:T(8,128)} %e_in.1, f32[3,3,8,24,128]{4,3,2,1,0:T(8,128)} %h_in.1, f32[3,8,24,128]{3,2,1,0:T(8,128)} %j_in.1, ...), custom_call_target="tpu_custom_call" | custom-call | tf_op jit(solution)/shard_map/window/pallas_call | solution.py:582
  27.0 1.2 %write_out.1 = (f32[3,3,8,24,128]{4,3,2,1,0:T(8,128)}, f32[3,3,8,24,128]{4,3,2,1,0:T(8,128)}) custom-call(f32[3,3,10,40,128]{4,3,2,1,0:T(8,128)S(1)} %get-tuple-element.4.e, f32[3,3,10,40,128]{4,3,2,1,0:T(8,128)S(1)} %get-tuple-element.5.h), custom_call_target="tpu_custom_call" | custom-call | tf_op jit(solution)/shard_map/write_out/pallas_call | solution.py:603

commit v3 on v2

--- a/solution.py
+++ b/solution.py
@@ -15,7 +15,7 @@
 
 PAD = 8
 MESH = pl.DeviceIdType.MESH
-UP, DOWN, DIAG_A, DIAG_B, RIGHT, LEFT = range(6)
+UP, DIAG, DOWN, SOURCE, CORNER, RIGHT, LEFT = range(7)
 
 
 def refine_weights(rows, columns, offset, cells):
@@ -70,18 +70,23 @@
     density,
     first_rows,
     s_up,
+    s_down,
+    mask_up,
     xlo,
     xhi,
     s_right,
     r_right,
     s_left,
     r_left,
-    r_diag_a,
-    r_diag_b,
+    s_corner,
+    r_corner,
     h_row,
     load_sem,
     send_sem,
-    recv_sem,
+    up_sem,
+    down_sem,
+    corner_sem,
+    narrow_sem,
     tile_sems,
 ):
     w = lax.axis_index("wide")
@@ -208,70 +213,73 @@
     def all_bytes(ref, k):
         return pltpu.make_async_copy(ref, ref, tile_sems.at[k])
 
-    def copies(s, r):
-        b = s % 2
-
-        def copy(kind, src, dst, to_w, to_n):
-            return pltpu.make_async_remote_copy(
-                src_ref=src,
-                dst_ref=dst,
-                send_sem=send_sem.at[r, kind],
-                recv_sem=recv_sem.at[b, r, kind],
-                device_id=(to_w, to_n),
-                device_id_type=MESH,
-            )
-
-        rows = 5 if s == 0 else 3
-        wide = [
-            (
-                has_down & has_right,
-                has_up & has_left,
-                copy(
-                    DIAG_A,
-                    E.at[r, 1, 1, pl.ds(PAD + Y - 1, 1), :],
-                    r_diag_a.at[b, r],
-                    w - 1,
-                    n + 1,
-                ),
-            ),
-            (
-                has_up & has_left,
-                has_down & has_right,
-                copy(
-                    DIAG_B, E.at[r, 0, X, pl.ds(PAD, 1), :], r_diag_b.at[b, r], w + 1, n - 1
-                ),
-            ),
-            (has_up, has_down, copy(UP, s_up.at[b, r], xlo.at[b, r], w + 1, n)),
-            (
-                has_down,
-                has_up,
-                copy(DOWN, E.at[r, pl.ds(1, 2), 1, own_y, :], xhi.at[b, r], w - 1, n),
-            ),
-        ]
-        narrow = [
-            (
-                has_right,
-                has_left,
-                copy(
-                    RIGHT,
-                    s_right.at[b, r, pl.ds(0, rows)],
-                    r_right.at[b, r, pl.ds(0, rows)],
-                    w,
-                    n + 1,
-                ),
-            ),
-            (has_left, has_right, copy(LEFT, s_left.at[b, r], r_left.at[b, r], w, n - 1)),
-        ]
-        return wide, narrow
-
-    def start(messages):
-        for sends, _, copy in messages:
-            pl.when(sends)(copy.start)
-
-    def finish(messages):
-        for sends, receives, copy in messages:
-            pl.when(receives)(copy.wait_recv)
-            pl.when(sends)(copy.wait_send)
+    def remote(src, dst, kind, arrived, to_w, to_n):
+        return pltpu.make_async_remote_copy(
+            src_ref=src,
+            dst_ref=dst,
+            send_sem=send_sem.at[kind],
+            recv_sem=arrived,
+            device_id=(to_w, to_n),
+            device_id_type=MESH,
+        )
+
+    planes = pl.ds(0, 2 * Y)
+    edge_row = pl.ds(2 * Y, 1)
+
+    def up_copy(s, r):
+        src, dst = s_up.at[s % 2, r, planes], xlo.at[s, r, planes]
+        return remote(src, dst, UP, up_sem.at[s, r], w + 1, n)
+
+    def diag_copy(s, r):
+        src, dst = s_up.at[s % 2, r, edge_row], xlo.at[s, r, edge_row]
+        return remote(src, dst, DIAG, up_sem.at[s, r], w + 1, n - 1)
+
+    def down_copy(s, r):
+        if s == 0:
+            src, kind = E.at[r, pl.ds(1, 2), 1, own_y, :], DOWN
+        else:
+            src, kind = s_down.at[s % 2, r], SOURCE
+        return remote(src, xhi.at[s, r], kind, down_sem.at[s, r], w - 1, n)
+
+    def corner_copy(s, r):
+        b = s % 2
+        to_w = w - 1 if s == 0 else w
+        return remote(s_corner.at[b, r], r_corner.at[b, r], CORNER, corner_sem.at[b, r], to_w, n + 1)
+
+    def sends_corner(s):
+        return has_right & (has_down if s == 0 else has_up)
+
+    def right_copy(s, r):
+        b = s % 2
+        rows = pl.ds(0, 5 if s == 0 else 3)
+        return remote(
+            s_right.at[b, r, rows], r_right.at[b, r, rows], RIGHT, narrow_sem.at[b, r, 0], w, n + 1
+        )
+
+    def left_copy(s, r):
+        b = s % 2
+        return remote(s_left.at[b, r], r_left.at[b, r], LEFT, narrow_sem.at[b, r, 1], w, n - 1)
+
+    def wait_all(there, ref, sem):
+        @pl.when(there)
+        def _():
+            pltpu.make_async_copy(ref, ref, sem).wait()
+
+    def finish_planes(s):
+        b = s % 2
+        wait_all(has_up, s_up.at[b, :, planes], send_sem.at[UP])
+        wait_all(has_up & has_left, s_up.at[b, :, edge_row], send_sem.at[DIAG])
+        rows = pl.ds(0, 5 if s == 0 else 3)
+        wait_all(has_right, s_right.at[b, :, rows], send_sem.at[RIGHT])
+        wait_all(has_left, s_left.at[b], send_sem.at[LEFT])
+        if s == 0:
+            wait_all(has_down, s_down.at[0], send_sem.at[DOWN])
+
+    def finish_source(s):
+        wait_all(has_down, s_down.at[s % 2], send_sem.at[SOURCE])
+
+    def finish_corner(s):
+        wait_all(sends_corner(s), s_corner.at[s % 2], send_sem.at[CORNER])
 
     last_row = lax.broadcasted_iota(jnp.int32, (Y, Z), 0) == Y - 1
 
@@ -287,18 +295,32 @@
         b = s % 2
         ex, ey, ez = (E[r, c, X, own_y, :] for c in range(3))
         beyond = jnp.where(last_row, 0.0, E[r, 0, X, pl.ds(PAD + 1, Y), :])
-        s_up[b, r, 0] = H[r, 1, X, own_y, :] - time_step * ((next_z(ex) - ex) + ez)
-        s_up[b, r, 1] = H[r, 2, X, own_y, :] + time_step * ((beyond - ex) + ey)
-        diag_a, diag_b, up, down = copies(s, r)[0]
+        s_up[b, r, edge_row, :] = E[r, 0, X, pl.ds(PAD, 1), :]
+        s_up[b, r, pl.ds(0, Y), :] = H[r, 1, X, own_y, :] - time_step * ((next_z(ex) - ex) + ez)
+        s_up[b, r, pl.ds(Y, Y), :] = H[r, 2, X, own_y, :] + time_step * ((beyond - ex) + ey)
+        if s > 0:
+            pl.when(has_up & has_left)(diag_copy(s, r).start)
+            pl.when(has_up)(up_copy(s, r).start)
+            return
+        s_corner[b, r] = E[r, 1, 1, pl.ds(PAD + Y - 1, 1), :]
         even = lax.rem(w, 2) == 0
 
-        @pl.when(even)
-        def _():
-            start([diag_a, down, diag_b, up])
-
-        @pl.when(jnp.logical_not(even))
-        def _():
-            start([diag_b, up, diag_a, down])
+        def go_down():
+            pl.when(sends_corner(0))(corner_copy(0, r).start)
+            pl.when(has_down)(down_copy(0, r).start)
+
+        pl.when(even)(go_down)
+        pl.when(has_up & has_left)(diag_copy(s, r).start)
+        pl.when(has_up)(up_copy(s, r).start)
+        pl.when(jnp.logical_not(even))(go_down)
+
+    def send_source(s, r):
+        b = s % 2
+        hx, hy, hz = (H[r, c, 1, own_y, :] for c in range(3))
+        left_hx = H[r, 0, 1, pl.ds(PAD - 1, Y), :]
+        s_down[b, r, 0] = (hx - last_z(hx)) - hz - J[1, 0]
+        s_down[b, r, 1] = hy - (hx - left_hx) - J[2, 0]
+        pl.when(has_down)(down_copy(s, r).start)
 
     def send_narrow(s, r):
         b = s % 2
@@ -310,11 +332,13 @@
                 s_right[b, r, 4, pl.ds(p, 1), :] = H[r, 2, p + 1, pl.ds(PAD + Y - 1, 1), :]
             s_left[b, r, 0, pl.ds(p, 1), :] = E[r, 0, p + 1, pl.ds(PAD, 1), :]
             s_left[b, r, 1, pl.ds(p, 1), :] = E[r, 2, p + 1, pl.ds(PAD, 1), :]
-        start(copies(s, r)[1])
+        pl.when(has_right)(right_copy(s, r).start)
+        pl.when(has_left)(left_copy(s, r).start)
 
     def receive_narrow(s, r):
         b = s % 2
-        finish(copies(s, r)[1])
+        pl.when(has_left)(right_copy(s, r).wait_recv)
+        pl.when(has_right)(left_copy(s, r).wait_recv)
 
         @pl.when(has_right)
         def _():
@@ -339,26 +363,48 @@
 
     def receive_wide(s, r):
         b = s % 2
-        finish(copies(s, r)[0])
+        both = pl.ds(0, 2 * Y + 1)
+        wait_all(has_down & has_right, xlo.at[s, r, both], up_sem.at[s, r])
+        wait_all(has_down & jnp.logical_not(has_right), xlo.at[s, r, planes], up_sem.at[s, r])
+        pl.when(has_up & has_left)(corner_copy(s, r).wait_recv)
 
         @pl.when(has_down)
         def _():
-            H[r, 1, 0, own_y, :] = xlo[b, r, 0] + time_step * E[r, 2, 1, own_y, :]
-            corner = jnp.broadcast_to(r_diag_b[b, r], (Y, Z))
-            corner = jnp.where(last_row & jnp.broadcast_to(has_right, (Y, Z)), corner, 0.0)
-            H[r, 2, 0, own_y, :] = xlo[b, r, 1] + time_step * (corner - E[r, 1, 1, own_y, :])
-
-        @pl.when(has_up)
-        def _():
-            E[r, 1, X + 1, own_y, :] = xhi[b, r, 0]
-            E[r, 2, X + 1, own_y, :] = xhi[b, r, 1]
+            edge = jnp.broadcast_to(xlo[s, r, edge_row, :], (Y, Z))
+            edge = jnp.where(last_row & jnp.broadcast_to(has_right, (Y, Z)), edge, 0.0)
+            low_y, low_z = xlo[s, r, pl.ds(0, Y), :], xlo[s, r, pl.ds(Y, Y), :]
+            H[r, 1, 0, own_y, :] = low_y + time_step * E[r, 2, 1, own_y, :]
+            H[r, 2, 0, own_y, :] = low_z + time_step * (edge - E[r, 1, 1, own_y, :])
+
+        if s == 0:
+
+            @pl.when(has_up)
+            def _():
+                down_copy(0, r).wait_recv()
+                E[r, 1, X + 1, own_y, :] = xhi[0, r, 0]
+                E[r, 2, X + 1, own_y, :] = xhi[0, r, 1]
 
         @pl.when(has_up & has_left)
         def _():
-            edge = h_row[r, 1, pl.ds(X - 1, 1), :]
-            edge = edge - time_step * r_diag_a[b, r]
+            edge = h_row[r, 1, pl.ds(X - 1, 1), :] - time_step * r_corner[b, r]
             h_row[r, 1, pl.ds(X - 1, 1), :] = edge
             H[r, 2, X, pl.ds(PAD - 1, 1), :] = edge
+
+    def receive_source(s, r):
+        b = s % 2
+
+        @pl.when(has_up)
+        def _():
+            down_copy(s, r).wait_recv()
+            k = coef[r, X]
+            hy, hz = H[r, 1, X, own_y, :], H[r, 2, X, own_y, :]
+            E[r, 1, X + 1, own_y, :] = E[r, 1, X + 1, own_y, :] + k * (xhi[s, r, 0] + hz)
+            E[r, 2, X + 1, own_y, :] = E[r, 2, X + 1, own_y, :] + k * (xhi[s, r, 1] - hy)
+
+        @pl.when(sends_corner(s))
+        def _():
+            s_corner[b, r] = E[r, 1, X + 1, pl.ds(PAD + Y - 1, 1), :]
+            corner_copy(s, r).start()
 
     def update_h(r, planes):
         above = pl.ds(PAD + 1, Y)
@@ -398,6 +444,11 @@
 
     for load in loads[3:]:
         load.wait()
+
+    @pl.loop(0, R)
+    def _(r):
+        receive_narrow(0, r)
+        update_h(r, inner_h)
 
     if L > 1:
         for k in range(2):
@@ -424,10 +475,29 @@
             chosen.at[lax.rem(j + d, P_)], found.at[j], 2, in_plane(d), n
         ).start()
 
+    mask_copy = pltpu.make_async_remote_copy(
+        src_ref=mask.at[0],
+        dst_ref=mask_up,
+        send_sem=tile_sems.at[6],
+        recv_sem=tile_sems.at[7],
+        device_id=(w - 1, n),
+        device_id_type=MESH,
+    )
+
+    if STEPS > 1:
+
+        @pl.loop(0, R)
+        def _(r):
+            send_source(1, r)
+
+    pl.when(has_down)(mask_copy.start)
+
+    finish_planes(0)
+
     @pl.loop(0, R)
     def _(r):
-        receive_narrow(0, r)
-        update_h(r, inner_h)
+        receive_wide(0, r)
+        update_h(r, (X,))
 
     if P_ > 1:
         for k in range(4, 6):
@@ -469,36 +539,48 @@
         (global_y >= box[2]) & (global_y < box[3]) & (global_z >= box[4]) & (global_z < box[5])
     )
 
-    @pl.loop(0, TR)
-    def _(c):
-        here = density[c]
-        for odd_plane in range(2):
-            value = 0.5 * (here + density[c + 1]) if odd_plane else here
-            x = 2 * c + odd_plane
-            global_x = w * X + x
-            x_inside = (global_x >= box[0]) & (global_x < box[1])
-            inside = inside_yz & jnp.broadcast_to(x_inside, (Y, Z))
-            background = jnp.where(mask[x] == 1, level1, level0)
-            for r, threshold in enumerate(thresholds):
-                low_end = math.tanh(sharpness * threshold)
-                scale = low_end + math.tanh(sharpness * (1.0 - threshold))
-                numer = low_end + jnp.tanh(sharpness * (value - threshold))
-                design = level0 + (numer / scale) * (level1 - level0)
-                coef[r, x] = time_step / jnp.where(inside, design, background)
+    def coefficients(value, x, background):
+        global_x = w * X + x
+        x_inside = (global_x >= box[0]) & (global_x < box[1])
+        inside = inside_yz & jnp.broadcast_to(x_inside, (Y, Z))
+        for r, threshold in enumerate(thresholds):
+            low_end = math.tanh(sharpness * threshold)
+            scale = low_end + math.tanh(sharpness * (1.0 - threshold))
+            numer = low_end + jnp.tanh(sharpness * (value - threshold))
+            design = level0 + (numer / scale) * (level1 - level0)
+            coef[r, x] = time_step / jnp.where(inside, design, background)
+
+    def own_coefficients(value, x):
+        coefficients(value, x, jnp.where(mask[x] == 1, level1, level0))
+
+    own_coefficients(density[0], 0)
+    own_coefficients(0.5 * (density[TR - 1] + density[TR]), X - 1)
 
     for s in range(STEPS):
         if s > 0:
+            finish_source(s)
 
             @pl.loop(0, R)
             def _(r):
                 receive_narrow(s, r)
                 update_h(r, inner_h)
+                if s < STEPS - 1:
+                    send_source(s + 1, r)
                 update_e(r, inner_e)
+
+            finish_corner(s - 1)
+
+            @pl.loop(0, R)
+            def _(r):
+                receive_source(s, r)
+
+            finish_planes(s)
 
         @pl.loop(0, R)
         def _(r):
-            receive_wide(s, r)
-            update_h(r, (X,))
+            if s > 0:
+                receive_wide(s, r)
+                update_h(r, (X,))
             update_e(r, edges)
             if s < STEPS - 1:
                 send_wide(s + 1, r)
@@ -507,11 +589,25 @@
 
         if s == 0:
 
+            @pl.loop(0, TR - 1)
+            def _(c):
+                own_coefficients(0.5 * (density[c] + density[c + 1]), 2 * c + 1)
+                own_coefficients(density[c + 1], 2 * c + 2)
+
+            @pl.when(has_up)
+            def _():
+                mask_copy.wait_recv()
+                coefficients(density[TR], X, jnp.where(mask_up[...] == 1, level1, level0))
+
+            pl.when(has_down)(mask_copy.wait_send)
+
             @pl.loop(0, R)
             def _(r):
                 update_e(r, inner_e)
                 if STEPS > 1:
                     send_narrow(1, r)
+
+    finish_corner(STEPS - 1)
 
 
 def write_out(e, h, e_out, h_out, sems):
@@ -557,15 +653,17 @@
         pltpu.VMEM((3, X, Y, Z), f32),
         pltpu.VMEM((HY, TR, HZ), f32),
         pltpu.VMEM((X, Y, Z), jnp.int32),
-        pltpu.VMEM((R, X, Y, Z), f32),
+        pltpu.VMEM((R, X + 1, Y, Z), f32),
         pltpu.VMEM((L, -(-(packed + half) // 8) * 8, Z), f32),
         pltpu.VMEM((P_, total, Z), f32),
         pltpu.VMEM((P_, total, Z), f32),
         pltpu.VMEM((TR + 1, Y, Z), f32),
         pltpu.VMEM((8, Z), f32),
+        pltpu.VMEM((2, R, 2 * Y + 8, Z), f32),
         pltpu.VMEM((2, R, 2, Y, Z), f32),
-        pltpu.VMEM((2, R, 2, Y, Z), f32),
-        pltpu.VMEM((2, R, 2, Y, Z), f32),
+        pltpu.VMEM((Y, Z), jnp.int32),
+        pltpu.VMEM((STEPS, R, 2 * Y + 8, Z), f32),
+        pltpu.VMEM((STEPS, R, 2, Y, Z), f32),
         pltpu.VMEM((2, R, 5, X, Z), f32),
         pltpu.VMEM((2, R, 5, X, Z), f32),
         pltpu.VMEM((2, R, 2, X, Z), f32),
@@ -574,9 +672,12 @@
         pltpu.VMEM((2, R, 1, Z), f32),
         pltpu.VMEM((R, 2, X, Z), f32),
         dma((8,)),
-        dma((R, 6)),
-        dma((2, R, 6)),
-        dma((6,)),
+        dma((7,)),
+        dma((STEPS, R)),
+        dma((STEPS, R)),
+        dma((2, R)),
+        dma((2, R, 2)),
+        dma((8,)),
     ]
     state = pltpu.VMEM((R, 3, X + 2, Y + 2 * PAD, Z), f32)
     e, h = pl.pallas_call(

time: 28.4 us -> 26.2 us (0.923)
  Pallas kernels: 27.6 us -> 25.2 us
    pallas_call x1, Pallas kernels: 26.4 us -> 24 us  [body(): pl.pallas_call(functools.partial(kernel, W, N), out_shape=(state, state),...]
where the time goes in v3:
time: 26.2 us; the launch traced here: 25.8 us
  Pallas kernels  25.2 us (96%)
  between operations  0.64 us (2%)
    pallas_call x1, Pallas kernels, body(): pl.pallas_call(functools.partial(kernel, W, N), out_shape=(state, state),...  24 us
    pallas_call x1, Pallas kernels, body(): pl.pallas_call(write_out, out_shape=(out, out), in_specs=[vmem] * 2, out_...  1.22 us

profile of v3, /device:TPU:0, one launch (start us, length us, event | category | flops | bytes accessed | tf_op | source)
XLA Modules:
  0.0 25.8 jit_solution(5034112728247667750)
XLA Ops:
  0.6 24.0 %window.1 = (f32[3,3,10,40,128]{4,3,2,1,0:T(8,128)S(1)}, f32[3,3,10,40,128]{4,3,2,1,0:T(8,128)S(1)}) custom-call(s32[16]{0:T(128)} %slabs_in.1, s32[6]{0:T(128)} %box_in.1, f32[2]{0:T(128)} %levels_in.1, f32[3,3,8,24,128]{4,3,2,1,0:T(8,128)} %e_in.1, f32[3,3,8,24,128]{4,3,2,1,0:T(8,128)} %h_in.1, f32[3,8,24,128]{3,2,1,0:T(8,128)} %j_in.1, ...), custom_call_target="tpu_custom_call" | custom-call | tf_op jit(solution)/shard_map/window/pallas_call | solution.py:683
  24.6 1.2 %write_out.1 = (f32[3,3,8,24,128]{4,3,2,1,0:T(8,128)}, f32[3,3,8,24,128]{4,3,2,1,0:T(8,128)}) custom-call(f32[3,3,10,40,128]{4,3,2,1,0:T(8,128)S(1)} %get-tuple-element.4.e, f32[3,3,10,40,128]{4,3,2,1,0:T(8,128)S(1)} %get-tuple-element.5.h), custom_call_target="tpu_custom_call" | custom-call | tf_op jit(solution)/shard_map/write_out/pallas_call | solution.py:704

commit v4 on v3

--- a/solution.py
+++ b/solution.py
@@ -265,10 +265,13 @@
         def _():
             pltpu.make_async_copy(ref, ref, sem).wait()
 
-    def finish_planes(s):
+    def finish_up(s):
         b = s % 2
         wait_all(has_up, s_up.at[b, :, planes], send_sem.at[UP])
         wait_all(has_up & has_left, s_up.at[b, :, edge_row], send_sem.at[DIAG])
+
+    def finish_narrow(s):
+        b = s % 2
         rows = pl.ds(0, 5 if s == 0 else 3)
         wait_all(has_right, s_right.at[b, :, rows], send_sem.at[RIGHT])
         wait_all(has_left, s_left.at[b], send_sem.at[LEFT])
@@ -291,120 +294,172 @@
         lane = lax.broadcasted_iota(jnp.int32, value.shape, 1)
         return jnp.where(lane == 0, 0.0, pltpu.roll(value, 1, 1))
 
-    def send_wide(s, r):
-        b = s % 2
-        ex, ey, ez = (E[r, c, X, own_y, :] for c in range(3))
-        beyond = jnp.where(last_row, 0.0, E[r, 0, X, pl.ds(PAD + 1, Y), :])
-        s_up[b, r, edge_row, :] = E[r, 0, X, pl.ds(PAD, 1), :]
-        s_up[b, r, pl.ds(0, Y), :] = H[r, 1, X, own_y, :] - time_step * ((next_z(ex) - ex) + ez)
-        s_up[b, r, pl.ds(Y, Y), :] = H[r, 2, X, own_y, :] + time_step * ((beyond - ex) + ey)
-        if s > 0:
-            pl.when(has_up & has_left)(diag_copy(s, r).start)
-            pl.when(has_up)(up_copy(s, r).start)
-            return
-        s_corner[b, r] = E[r, 1, 1, pl.ds(PAD + Y - 1, 1), :]
-        even = lax.rem(w, 2) == 0
-
-        def go_down():
-            pl.when(sends_corner(0))(corner_copy(0, r).start)
-            pl.when(has_down)(down_copy(0, r).start)
-
-        pl.when(even)(go_down)
+    reals = range(R)
+
+    def send_up(s):
+        b = s % 2
+        for r in reals:
+            ex, ey, ez = (E[r, c, X, own_y, :] for c in range(3))
+            beyond = jnp.where(last_row, 0.0, E[r, 0, X, pl.ds(PAD + 1, Y), :])
+            low_y = H[r, 1, X, own_y, :] - time_step * ((next_z(ex) - ex) + ez)
+            low_z = H[r, 2, X, own_y, :] + time_step * ((beyond - ex) + ey)
+            s_up[b, r, edge_row, :] = E[r, 0, X, pl.ds(PAD, 1), :]
+            s_up[b, r, pl.ds(0, Y), :] = low_y
+            s_up[b, r, pl.ds(Y, Y), :] = low_z
+
+    def start_up(s, r):
         pl.when(has_up & has_left)(diag_copy(s, r).start)
         pl.when(has_up)(up_copy(s, r).start)
-        pl.when(jnp.logical_not(even))(go_down)
-
-    def send_source(s, r):
-        b = s % 2
-        hx, hy, hz = (H[r, c, 1, own_y, :] for c in range(3))
-        left_hx = H[r, 0, 1, pl.ds(PAD - 1, Y), :]
-        s_down[b, r, 0] = (hx - last_z(hx)) - hz - J[1, 0]
-        s_down[b, r, 1] = hy - (hx - left_hx) - J[2, 0]
-        pl.when(has_down)(down_copy(s, r).start)
-
-    def send_narrow(s, r):
-        b = s % 2
-        for p in range(X):
-            for c in range(3):
-                s_right[b, r, c, pl.ds(p, 1), :] = E[r, c, p + 1, pl.ds(PAD + Y - 1, 1), :]
-            if s == 0:
-                s_right[b, r, 3, pl.ds(p, 1), :] = H[r, 0, p + 1, pl.ds(PAD + Y - 1, 1), :]
-                s_right[b, r, 4, pl.ds(p, 1), :] = H[r, 2, p + 1, pl.ds(PAD + Y - 1, 1), :]
-            s_left[b, r, 0, pl.ds(p, 1), :] = E[r, 0, p + 1, pl.ds(PAD, 1), :]
-            s_left[b, r, 1, pl.ds(p, 1), :] = E[r, 2, p + 1, pl.ds(PAD, 1), :]
-        pl.when(has_right)(right_copy(s, r).start)
-        pl.when(has_left)(left_copy(s, r).start)
-
-    def receive_narrow(s, r):
-        b = s % 2
-        pl.when(has_left)(right_copy(s, r).wait_recv)
-        pl.when(has_right)(left_copy(s, r).wait_recv)
+
+    def send_first():
+        send_up(0)
+        for r in reals:
+            s_corner[0, r] = E[r, 1, 1, pl.ds(PAD + Y - 1, 1), :]
+        even = lax.rem(w, 2) == 0
+
+        @pl.loop(0, R)
+        def _(r):
+            def go_down():
+                pl.when(sends_corner(0))(corner_copy(0, r).start)
+                pl.when(has_down)(down_copy(0, r).start)
+
+            pl.when(even)(go_down)
+            start_up(0, r)
+            pl.when(jnp.logical_not(even))(go_down)
+
+    def send_source(s):
+        b = s % 2
+        for r in reals:
+            hx, hy, hz = (H[r, c, 1, own_y, :] for c in range(3))
+            left_hx = H[r, 0, 1, pl.ds(PAD - 1, Y), :]
+            s_down[b, r, 0] = (hx - last_z(hx)) - hz - J[1, 0]
+            s_down[b, r, 1] = hy - (hx - left_hx) - J[2, 0]
+
+        @pl.when(has_down)
+        def _():
+            for r in reals:
+                down_copy(s, r).start()
+
+    def send_narrow(s):
+        b = s % 2
 
         @pl.when(has_right)
         def _():
-            for p in range(X):
-                E[r, 0, p + 1, pl.ds(PAD + Y, 1), :] = r_left[b, r, 0, pl.ds(p, 1), :]
-                E[r, 2, p + 1, pl.ds(PAD + Y, 1), :] = r_left[b, r, 1, pl.ds(p, 1), :]
+            for r in reals:
+                last = pl.ds(PAD + Y - 1, 1)
+                for p in range(X):
+                    for c in range(3):
+                        s_right[b, r, c, pl.ds(p, 1), :] = E[r, c, p + 1, last, :]
+                    if s == 0:
+                        s_right[b, r, 3, pl.ds(p, 1), :] = H[r, 0, p + 1, last, :]
+                        s_right[b, r, 4, pl.ds(p, 1), :] = H[r, 2, p + 1, last, :]
+                right_copy(s, r).start()
 
         @pl.when(has_left)
         def _():
-            ex, ey, ez = (r_right[b, r, c] for c in range(3))
-            if s == 0:
-                hx, hz = r_right[b, r, 3], r_right[b, r, 4]
-            else:
-                hx, hz = h_row[r, 0], h_row[r, 1]
+            for r in reals:
+                for p in range(X):
+                    s_left[b, r, 0, pl.ds(p, 1), :] = E[r, 0, p + 1, pl.ds(PAD, 1), :]
+                    s_left[b, r, 1, pl.ds(p, 1), :] = E[r, 2, p + 1, pl.ds(PAD, 1), :]
+                left_copy(s, r).start()
+
+    def receive_narrow(s):
+        b = s % 2
+
+        @pl.when(has_right)
+        def _():
+            for r in reals:
+                left_copy(s, r).wait_recv()
+            for r in reals:
+                for p in range(X):
+                    E[r, 0, p + 1, pl.ds(PAD + Y, 1), :] = r_left[b, r, 0, pl.ds(p, 1), :]
+                    E[r, 2, p + 1, pl.ds(PAD + Y, 1), :] = r_left[b, r, 1, pl.ds(p, 1), :]
+
+        @pl.when(has_left)
+        def _():
+            for r in reals:
+                right_copy(s, r).wait_recv()
             plane = lax.broadcasted_iota(jnp.int32, (X, Z), 0)
-            ey_up = jnp.where(plane == X - 1, 0.0, pltpu.roll(ey, X - 1, 0))
-            h_row[r, 0] = hx - time_step * ((s_left[b, r, 1] - ez) - (next_z(ey) - ey))
-            h_row[r, 1] = hz - time_step * ((ey_up - ey) - (s_left[b, r, 0] - ex))
-            for p in range(X):
-                H[r, 0, p + 1, pl.ds(PAD - 1, 1), :] = h_row[r, 0, pl.ds(p, 1), :]
-                H[r, 2, p + 1, pl.ds(PAD - 1, 1), :] = h_row[r, 1, pl.ds(p, 1), :]
-
-    def receive_wide(s, r):
-        b = s % 2
+            for r in reals:
+                ex, ey, ez = (r_right[b, r, c] for c in range(3))
+                if s == 0:
+                    hx, hz = r_right[b, r, 3], r_right[b, r, 4]
+                else:
+                    hx, hz = h_row[r, 0], h_row[r, 1]
+                ey_up = jnp.where(plane == X - 1, 0.0, pltpu.roll(ey, X - 1, 0))
+                own_ex, own_ez = s_left[b, r, 0], s_left[b, r, 1]
+                h_row[r, 0] = hx - time_step * ((own_ez - ez) - (next_z(ey) - ey))
+                h_row[r, 1] = hz - time_step * ((ey_up - ey) - (own_ex - ex))
+            for r in reals:
+                for p in range(X):
+                    H[r, 0, p + 1, pl.ds(PAD - 1, 1), :] = h_row[r, 0, pl.ds(p, 1), :]
+                    H[r, 2, p + 1, pl.ds(PAD - 1, 1), :] = h_row[r, 1, pl.ds(p, 1), :]
+
+    def receive_up(s):
         both = pl.ds(0, 2 * Y + 1)
-        wait_all(has_down & has_right, xlo.at[s, r, both], up_sem.at[s, r])
-        wait_all(has_down & jnp.logical_not(has_right), xlo.at[s, r, planes], up_sem.at[s, r])
-        pl.when(has_up & has_left)(corner_copy(s, r).wait_recv)
+
+        @pl.when(has_down & has_right)
+        def _():
+            for r in reals:
+                ref = xlo.at[s, r, both]
+                pltpu.make_async_copy(ref, ref, up_sem.at[s, r]).wait()
+
+        @pl.when(has_down & jnp.logical_not(has_right))
+        def _():
+            for r in reals:
+                ref = xlo.at[s, r, planes]
+                pltpu.make_async_copy(ref, ref, up_sem.at[s, r]).wait()
 
         @pl.when(has_down)
         def _():
-            edge = jnp.broadcast_to(xlo[s, r, edge_row, :], (Y, Z))
-            edge = jnp.where(last_row & jnp.broadcast_to(has_right, (Y, Z)), edge, 0.0)
-            low_y, low_z = xlo[s, r, pl.ds(0, Y), :], xlo[s, r, pl.ds(Y, Y), :]
-            H[r, 1, 0, own_y, :] = low_y + time_step * E[r, 2, 1, own_y, :]
-            H[r, 2, 0, own_y, :] = low_z + time_step * (edge - E[r, 1, 1, own_y, :])
+            for r in reals:
+                edge = jnp.broadcast_to(xlo[s, r, edge_row, :], (Y, Z))
+                edge = jnp.where(last_row & jnp.broadcast_to(has_right, (Y, Z)), edge, 0.0)
+                low_y, low_z = xlo[s, r, pl.ds(0, Y), :], xlo[s, r, pl.ds(Y, Y), :]
+                H[r, 1, 0, own_y, :] = low_y + time_step * E[r, 2, 1, own_y, :]
+                H[r, 2, 0, own_y, :] = low_z + time_step * (edge - E[r, 1, 1, own_y, :])
+
+    def receive_corner(s):
+        b = s % 2
+
+        @pl.when(has_up & has_left)
+        def _():
+            for r in reals:
+                corner_copy(s, r).wait_recv()
+            for r in reals:
+                edge = h_row[r, 1, pl.ds(X - 1, 1), :] - time_step * r_corner[b, r]
+                h_row[r, 1, pl.ds(X - 1, 1), :] = edge
+                H[r, 2, X, pl.ds(PAD - 1, 1), :] = edge
 
         if s == 0:
 
             @pl.when(has_up)
             def _():
-                down_copy(0, r).wait_recv()
-                E[r, 1, X + 1, own_y, :] = xhi[0, r, 0]
-                E[r, 2, X + 1, own_y, :] = xhi[0, r, 1]
-
-        @pl.when(has_up & has_left)
-        def _():
-            edge = h_row[r, 1, pl.ds(X - 1, 1), :] - time_step * r_corner[b, r]
-            h_row[r, 1, pl.ds(X - 1, 1), :] = edge
-            H[r, 2, X, pl.ds(PAD - 1, 1), :] = edge
-
-    def receive_source(s, r):
+                for r in reals:
+                    down_copy(0, r).wait_recv()
+                for r in reals:
+                    E[r, 1, X + 1, own_y, :] = xhi[0, r, 0]
+                    E[r, 2, X + 1, own_y, :] = xhi[0, r, 1]
+
+    def receive_source(s):
         b = s % 2
 
         @pl.when(has_up)
         def _():
-            down_copy(s, r).wait_recv()
-            k = coef[r, X]
-            hy, hz = H[r, 1, X, own_y, :], H[r, 2, X, own_y, :]
-            E[r, 1, X + 1, own_y, :] = E[r, 1, X + 1, own_y, :] + k * (xhi[s, r, 0] + hz)
-            E[r, 2, X + 1, own_y, :] = E[r, 2, X + 1, own_y, :] + k * (xhi[s, r, 1] - hy)
+            for r in reals:
+                down_copy(s, r).wait_recv()
+            for r in reals:
+                k = coef[r, X]
+                hy, hz = H[r, 1, X, own_y, :], H[r, 2, X, own_y, :]
+                ey = E[r, 1, X + 1, own_y, :] + k * (xhi[s, r, 0] + hz)
+                E[r, 1, X + 1, own_y, :] = ey
+                E[r, 2, X + 1, own_y, :] = E[r, 2, X + 1, own_y, :] + k * (xhi[s, r, 1] - hy)
+                s_corner[b, r] = ey[Y - 1 : Y]
 
         @pl.when(sends_corner(s))
         def _():
-            s_corner[b, r] = E[r, 1, X + 1, pl.ds(PAD + Y - 1, 1), :]
-            corner_copy(s, r).start()
+            for r in reals:
+                corner_copy(s, r).start()
 
     def update_h(r, planes):
         above = pl.ds(PAD + 1, Y)
@@ -429,25 +484,18 @@
 
     inner_h = range(1, X)
     inner_e = range(2, X)
-    edges = (1, X)
 
     loads[1].wait()
     loads[2].wait()
 
-    @pl.loop(0, R)
-    def _(r):
-        send_wide(0, r)
-
-    @pl.loop(0, R)
-    def _(r):
-        send_narrow(0, r)
+    send_first()
+    send_narrow(0)
 
     for load in loads[3:]:
         load.wait()
 
-    @pl.loop(0, R)
-    def _(r):
-        receive_narrow(0, r)
+    receive_narrow(0)
+    for r in reals:
         update_h(r, inner_h)
 
     if L > 1:
@@ -485,19 +533,17 @@
     )
 
     if STEPS > 1:
-
-        @pl.loop(0, R)
-        def _(r):
-            send_source(1, r)
+        send_source(1)
 
     pl.when(has_down)(mask_copy.start)
 
-    finish_planes(0)
-
-    @pl.loop(0, R)
-    def _(r):
-        receive_wide(0, r)
+    finish_up(0)
+    finish_narrow(0)
+
+    receive_corner(0)
+    for r in reals:
         update_h(r, (X,))
+    receive_up(0)
 
     if P_ > 1:
         for k in range(4, 6):
@@ -553,59 +599,59 @@
     def own_coefficients(value, x):
         coefficients(value, x, jnp.where(mask[x] == 1, level1, level0))
 
+    own_coefficients(0.5 * (density[TR - 1] + density[TR]), X - 1)
+
+    def update_top(s):
+        if s > 0:
+            receive_corner(s)
+            for r in reals:
+                update_h(r, (X,))
+        for r in reals:
+            update_e(r, (X,))
+        if s < STEPS - 1:
+            send_up(s + 1)
+            for r in reals:
+                start_up(s + 1, r)
+
+    update_top(0)
+
     own_coefficients(density[0], 0)
-    own_coefficients(0.5 * (density[TR - 1] + density[TR]), X - 1)
-
-    for s in range(STEPS):
-        if s > 0:
-            finish_source(s)
-
-            @pl.loop(0, R)
-            def _(r):
-                receive_narrow(s, r)
-                update_h(r, inner_h)
-                if s < STEPS - 1:
-                    send_source(s + 1, r)
-                update_e(r, inner_e)
-
-            finish_corner(s - 1)
-
-            @pl.loop(0, R)
-            def _(r):
-                receive_source(s, r)
-
-            finish_planes(s)
-
-        @pl.loop(0, R)
-        def _(r):
-            if s > 0:
-                receive_wide(s, r)
-                update_h(r, (X,))
-            update_e(r, edges)
-            if s < STEPS - 1:
-                send_wide(s + 1, r)
-                if s > 0:
-                    send_narrow(s + 1, r)
-
-        if s == 0:
-
-            @pl.loop(0, TR - 1)
-            def _(c):
-                own_coefficients(0.5 * (density[c] + density[c + 1]), 2 * c + 1)
-                own_coefficients(density[c + 1], 2 * c + 2)
-
-            @pl.when(has_up)
-            def _():
-                mask_copy.wait_recv()
-                coefficients(density[TR], X, jnp.where(mask_up[...] == 1, level1, level0))
-
-            pl.when(has_down)(mask_copy.wait_send)
-
-            @pl.loop(0, R)
-            def _(r):
-                update_e(r, inner_e)
-                if STEPS > 1:
-                    send_narrow(1, r)
+    for c in range(TR - 1):
+        own_coefficients(0.5 * (density[c] + density[c + 1]), 2 * c + 1)
+        own_coefficients(density[c + 1], 2 * c + 2)
+    for r in reals:
+        update_e(r, range(1, X))
+    if STEPS > 1:
+        send_narrow(1)
+
+    @pl.when(has_up)
+    def _():
+        mask_copy.wait_recv()
+        coefficients(density[TR], X, jnp.where(mask_up[...] == 1, level1, level0))
+
+    pl.when(has_down)(mask_copy.wait_send)
+
+    for s in range(1, STEPS):
+        finish_source(s)
+        receive_narrow(s)
+        for r in reals:
+            update_h(r, (1,))
+        if s < STEPS - 1:
+            send_source(s + 1)
+        for r in reals:
+            update_h(r, range(2, X))
+        for r in reals:
+            update_e(r, inner_e)
+        finish_corner(s - 1)
+        receive_source(s)
+        finish_up(s)
+        update_top(s)
+        finish_narrow(s)
+        receive_up(s)
+        for r in reals:
+            update_e(r, (1,))
+        if s < STEPS - 1:
+            send_narrow(s + 1)
 
     finish_corner(STEPS - 1)
 

time: 26.2 us -> 25.4 us (0.969)
  the two profiles are of different devices: /device:TPU:0 before, /device:TPU:7 now
where the time goes in v4:
time: 25.4 us; the launch traced here: 25.3 us
  Pallas kernels  24.6 us (97%)
  between operations  0.64 us (3%)
    pallas_call x1, Pallas kernels, body(): pl.pallas_call(functools.partial(kernel, W, N), out_shape=(state, state),...  23.4 us
    pallas_call x1, Pallas kernels, body(): pl.pallas_call(write_out, out_shape=(out, out), in_specs=[vmem] * 2, out_...  1.22 us

profile of v4, /device:TPU:7, one launch (start us, length us, event | category | flops | bytes accessed | tf_op | source)
XLA Modules:
  0.0 25.3 jit_solution(3769922781954402627)
XLA Ops:
  0.6 23.4 %window.1 = (f32[3,3,10,40,128]{4,3,2,1,0:T(8,128)S(1)}, f32[3,3,10,40,128]{4,3,2,1,0:T(8,128)S(1)}) custom-call(s32[16]{0:T(128)} %slabs_in.1, s32[6]{0:T(128)} %box_in.1, f32[2]{0:T(128)} %levels_in.1, f32[3,3,8,24,128]{4,3,2,1,0:T(8,128)} %e_in.1, f32[3,3,8,24,128]{4,3,2,1,0:T(8,128)} %h_in.1, f32[3,8,24,128]{3,2,1,0:T(8,128)} %j_in.1, ...), custom_call_target="tpu_custom_call" | custom-call | tf_op jit(solution)/shard_map/window/pallas_call | solution.py:729
  24.1 1.2 %write_out.1 = (f32[3,3,8,24,128]{4,3,2,1,0:T(8,128)}, f32[3,3,8,24,128]{4,3,2,1,0:T(8,128)}) custom-call(f32[3,3,10,40,128]{4,3,2,1,0:T(8,128)S(1)} %get-tuple-element.4.e, f32[3,3,10,40,128]{4,3,2,1,0:T(8,128)S(1)} %get-tuple-element.5.h), custom_call_target="tpu_custom_call" | custom-call | tf_op jit(solution)/shard_map/write_out/pallas_call | solution.py:750

commit v5 on v4

--- a/solution.py
+++ b/solution.py
@@ -112,8 +112,6 @@
         pltpu.make_async_copy(box_in, box, load_sem.at[6]),
         pltpu.make_async_copy(levels_in, levels, load_sem.at[7]),
     ]
-    for load in loads:
-        load.start()
 
     has_up = w < W - 1
     has_down = w > 0
@@ -125,6 +123,7 @@
             (line.shape[1] - packed, Z), jnp.float32
         )
 
+    loads[0].start()
     barrier = pltpu.get_barrier_semaphore()
 
     def greet(to_w, to_n):
@@ -160,6 +159,9 @@
         def _():
             for d in range(L):
                 greet(along_line(d), to_n)
+
+    for load in loads[1:]:
+        load.start()
 
     zero_plane = jnp.zeros((Y + 2 * PAD, Z), jnp.float32)
     zero_tile = jnp.zeros((PAD, Z), jnp.float32)
@@ -645,11 +647,23 @@
         finish_corner(s - 1)
         receive_source(s)
         finish_up(s)
-        update_top(s)
         finish_narrow(s)
+        if s == 1 and STEPS > 2:
+            update_top(s)
         receive_up(s)
-        for r in reals:
-            update_e(r, (1,))
+        if s == 1 and STEPS > 2:
+            for r in reals:
+                update_e(r, (1,))
+        else:
+            receive_corner(s)
+            for r in reals:
+                update_h(r, (X,))
+            for r in reals:
+                update_e(r, (1, X))
+            if s < STEPS - 1:
+                send_up(s + 1)
+                for r in reals:
+                    start_up(s + 1, r)
         if s < STEPS - 1:
             send_narrow(s + 1)
 

time: 25.4 us -> 25.3 us (level)
  the two profiles are of different devices: /device:TPU:7 before, /device:TPU:10 now
where the time goes in v5:
time: 25.3 us; the launch traced here: 25.2 us
  Pallas kernels  24.5 us (97%)
  between operations  0.64 us (3%)
    pallas_call x1, Pallas kernels, body(): pl.pallas_call(functools.partial(kernel, W, N), out_shape=(state, state),...  23.3 us
    pallas_call x1, Pallas kernels, body(): pl.pallas_call(write_out, out_shape=(out, out), in_specs=[vmem] * 2, out_...  1.22 us

profile of v5, /device:TPU:10, one launch (start us, length us, event | category | flops | bytes accessed | tf_op | source)
XLA Modules:
  0.0 25.2 jit_solution(230648750047223368)
XLA Ops:
  0.6 23.3 %window.1 = (f32[3,3,10,40,128]{4,3,2,1,0:T(8,128)S(1)}, f32[3,3,10,40,128]{4,3,2,1,0:T(8,128)S(1)}) custom-call(s32[16]{0:T(128)} %slabs_in.1, s32[6]{0:T(128)} %box_in.1, f32[2]{0:T(128)} %levels_in.1, f32[3,3,8,24,128]{4,3,2,1,0:T(8,128)} %e_in.1, f32[3,3,8,24,128]{4,3,2,1,0:T(8,128)} %h_in.1, f32[3,8,24,128]{3,2,1,0:T(8,128)} %j_in.1, ...), custom_call_target="tpu_custom_call" | custom-call | tf_op jit(solution)/shard_map/window/pallas_call | solution.py:743
  24.0 1.2 %write_out.1 = (f32[3,3,8,24,128]{4,3,2,1,0:T(8,128)}, f32[3,3,8,24,128]{4,3,2,1,0:T(8,128)}) custom-call(f32[3,3,10,40,128]{4,3,2,1,0:T(8,128)S(1)} %get-tuple-element.4.e, f32[3,3,10,40,128]{4,3,2,1,0:T(8,128)S(1)} %get-tuple-element.5.h), custom_call_target="tpu_custom_call" | custom-call | tf_op jit(solution)/shard_map/write_out/pallas_call | solution.py:764
